TPU v7x, 32 devices: a whole 2x2x4 slice. The times are simulated.
32 devices in a mesh: dp: 8 (over z, x), ctx: 4 (over y, core).
Axes of the slice: x: 2, y: 2, z: 4, core: 2. Of those that a mesh axis runs over, the one named last changes fastest.
Arguments:
- queries: bfloat16 [8, 1024, 2048], P('dp', 'ctx'), may hold values from -100 to 100
- keys: bfloat16 [8, 1024, 512], P('dp', 'ctx'), may hold values from -4 to 4
- values: bfloat16 [8, 1024, 512], P('dp', 'ctx'), may hold values from -6 to 6
- segments: int32 [8, 1024], P('dp', 'ctx'), may hold values from 0 to 7, never falling along the last dimension, each value on 1 to 512 neighbouring positions
Outputs:
- attended: bfloat16 [8, 1024, 2048], P('dp', 'ctx')
Inputs may be any that keep to these rules, and one draw needn't show every extreme that they name: `segments`: document numbers never fall along a packed batch, every one of the 8 documents is present, and each document has at most 512 tokens; some document has exactly 512.
All inputs are finite; a program needn't handle non-finite values.
Results may differ from a plain program's by a relative error of at most 0.0053.
Values may be sent and summed in bfloat16 or wider, within the bound.
No kernel may reach another device: no remote copies, remote signals or barrier semaphores. Data moves between devices by JAX's collectives and lax.ppermute only.
A program may use at most 192 MiB of HBM per device.

v0:
```python
import jax
import jax.numpy as jnp
from jax import lax
from jax.sharding import PartitionSpec as P

HQ = 16
HK = 4
HD = 128


rope_theta = 500000.0


def entering(value, axis, join, neutral):
    count, mine = (lax.axis_size(axis), lax.axis_index(axis))
    pieces = jax.tree.map(lambda part: lax.all_gather(part, axis), value)
    running = jax.tree.map(
        lambda part, zero: jnp.full_like(part, 0) + jnp.asarray(zero, part.dtype), value, neutral
    )

    def hop(position, running):
        longer = join(running, jax.tree.map(lambda part: part[position], pieces))
        return jax.tree.map(lambda new, old: jnp.where(position < mine, new, old), longer, running)

    return lax.fori_loop(0, count - 1, hop, running)


def from_behind(block, axis, distance):
    devices = range(lax.axis_size(axis))
    route = [(i - distance, i) for i in devices if i - distance in devices]
    return lax.ppermute(block, axis, route)


def rotate(values_in, positions, heads, head_dim):
    rows = values_in.shape[0]
    half_dim = head_dim // 2
    split = values_in.astype(jnp.float32).reshape(rows, heads, head_dim)
    inv_freq = jnp.exp(
        -jnp.log(rope_theta) * 2.0 * jnp.arange(half_dim, dtype=jnp.float32) / head_dim
    )
    angles = positions.astype(jnp.float32)[:, None] * inv_freq[None, :]
    cosine_part = jnp.cos(angles)[:, None, :]
    sine_part = jnp.sin(angles)[:, None, :]
    first_half = split[..., :half_dim]
    second_half = split[..., half_dim:]
    turned = jnp.concatenate(
        [
            first_half * cosine_part - second_half * sine_part,
            second_half * cosine_part + first_half * sine_part,
        ],
        axis=-1,
    )
    return turned.reshape(rows, heads * head_dim).astype(jnp.bfloat16)


def join_runs(earlier, later):
    joined_uniform = earlier[3] * later[3] * (earlier[1] == later[0]).astype(jnp.int32)
    joined_trail = jnp.where(
        (later[3] == 1) & (later[0] == earlier[1]), earlier[2] + later[2], later[2]
    )
    joined = (earlier[0], later[1], joined_trail, joined_uniform, jnp.int32(0))
    return tuple(
        (
            jnp.where(
                earlier[4] == 1, later_part, jnp.where(later[4] == 1, earlier_part, joined_part)
            )
            for earlier_part, later_part, joined_part in zip(earlier, later, joined)
        )
    )


def attend_piece(
    state_in, key_piece, value_piece, key_segs, key_start, query_heads, query_segs, query_index
):
    run_max, run_sum, accumulated = state_in
    width = key_piece.shape[0]
    kv_heads = query_heads.shape[1]
    head_dim = query_heads.shape[3]
    key_heads = key_piece.reshape(width, kv_heads, head_dim)
    value_heads = value_piece.reshape(width, kv_heads, head_dim)
    key_index = key_start + jnp.arange(width, dtype=jnp.int32)
    live_mask = (
        (key_segs[None, :] == query_segs[:, None])
        & (key_index[None, :] <= query_index[:, None])
        & (key_index[None, :] >= 0)
    )
    scores = jnp.einsum(
        "thgd,shd->hgts", query_heads, key_heads, preferred_element_type=jnp.float32
    ) / jnp.sqrt(jnp.float32(head_dim))
    scores = jnp.where(live_mask, scores, jnp.float32(-1e30))
    new_max = jnp.maximum(run_max, jnp.max(scores, axis=-1))
    weights = jnp.where(live_mask, jnp.exp(scores - new_max[..., None]), jnp.float32(0.0))
    rescale = jnp.exp(run_max - new_max)
    new_sum = run_sum * rescale + jnp.sum(weights, axis=-1)
    weighted = jnp.einsum(
        "hgts,shd->thgd",
        weights.astype(jnp.bfloat16),
        value_heads,
        preferred_element_type=jnp.float32,
    )
    new_acc = accumulated * jnp.transpose(rescale, (2, 0, 1))[..., None] + weighted
    return (new_max, new_sum, new_acc)


def body(queries, keys, values, segments):
    tok_rows = segments.shape[1]
    cycle_size = lax.axis_size("ctx")
    cycle_index = lax.axis_index("ctx")
    seg_ids = segments[0]
    index_all = jnp.arange(tok_rows, dtype=jnp.int32)
    previous = jnp.concatenate([seg_ids[:1] - 1, seg_ids[:-1]])
    run_start = lax.cummax(jnp.where(seg_ids != previous, index_all, 0), axis=0)
    local_pos = index_all - run_start
    summary = (
        seg_ids[0],
        seg_ids[-1],
        jnp.int32(tok_rows) - run_start[-1],
        (seg_ids[0] == seg_ids[-1]).astype(jnp.int32),
        jnp.int32(0),
    )
    identity = (jnp.int32(0), jnp.int32(0), jnp.int32(0), jnp.int32(1), jnp.int32(1))
    prefix = entering(summary, "ctx", join_runs, identity)
    carried = jnp.where((prefix[4] == 0) & (prefix[1] == seg_ids[0]), prefix[2], 0)
    positions = jnp.where(run_start == 0, local_pos + carried, local_pos)
    head_dim = HD
    q_heads_all = HQ
    kv_heads = HK
    group_size = q_heads_all // kv_heads
    rot_q = rotate(queries[0], positions, q_heads_all, head_dim)
    rot_k = rotate(keys[0], positions, kv_heads, head_dim)
    query_heads = rot_q.reshape(tok_rows, kv_heads, group_size, head_dim)
    query_index = cycle_index * tok_rows + index_all
    initial = (
        jnp.full((kv_heads, group_size, tok_rows), -1e30, jnp.float32),
        jnp.zeros((kv_heads, group_size, tok_rows), jnp.float32),
        jnp.zeros((tok_rows, kv_heads, group_size, head_dim), jnp.float32),
    )
    own_state = attend_piece(
        initial,
        rot_k,
        values[0],
        seg_ids,
        cycle_index * tok_rows,
        query_heads,
        seg_ids,
        query_index,
    )

    def pass_step(step_index, loop_state):
        state_now, travelling = loop_state
        arrived = from_behind((travelling[0], travelling[1], travelling[2]), "ctx", 1)
        updated = attend_piece(
            state_now,
            arrived[0],
            arrived[1],
            arrived[2],
            (cycle_index - step_index) * tok_rows,
            query_heads,
            seg_ids,
            query_index,
        )
        return (updated, arrived)

    final_state, unused_piece = lax.fori_loop(
        1, cycle_size // 2 + 1, pass_step, (own_state, (rot_k, values[0], seg_ids))
    )
    run_max, run_sum, accumulated = final_state
    result = accumulated / jnp.transpose(run_sum, (2, 0, 1))[..., None]
    attended = result.reshape(tok_rows, q_heads_all * head_dim).astype(jnp.bfloat16)[None]
    return attended


def solution(mesh):
    placed = (P("dp", "ctx", None), P("dp", "ctx", None), P("dp", "ctx", None), P("dp", "ctx"))
    return jax.shard_map(
        body, mesh=mesh, in_specs=placed, out_specs=P("dp", "ctx", None), check_vma=False
    )
```

profile of v0, /device:TPU:1, one launch (start us, length us, event | category | flops | bytes accessed | tf_op | source)
XLA Modules:
  0.0 91.6 jit_solution(15335493625381826933)
XLA Ops:
  0.0 1.3 %fusion.41 = (s32[1,1]{1,0:T(1,128)}, s32[1,1]{1,0:T(1,128)}) fusion(s32[1,256]{1,0:T(1,128)} %param.11), kind=kLoop, calls=%fused_computation.70 | loop fusion | bytes 16 | tf_op jit(solution)/shard_map/slice | solution.py:116
  2.0 0.8 compare_select_fusion.1
  2.8 0.3 reduce-window.9
  3.4 1.3 %dynamic-slice = u32[1]{0:T(128)} dynamic-slice(u32[32]{0:T(128)} %constant.119, u32[]{:T(128)S(6)} %add.134), dynamic_slice_sizes={1} | dynamic-slice | bytes 12
  4.7 0.8 subtract_dynamic-update-slice_fusion
  6.7 0.7 dynamic-update-slice.3
  7.5 1.3 %bitcast_dynamic-update-slice_fusion = s32[4]{0:T(128)S(1)} fusion(s32[4]{0:T(128)S(1)} %broadcast.133.clone.4, u32[]{:T(128)} %bitcast.13, s32[1,1]{1,0:T(1,128)} %get-tuple-element.457), kind=kLoop, calls=%fused_computation.60 | loop fusion | bytes 24
  8.8 1.2 %bitcast_dynamic-update-slice_fusion.1 = s32[4]{0:T(128)S(1)} fusion(s32[4]{0:T(128)S(1)} %broadcast.133.clone, u32[]{:T(128)} %bitcast.13, s32[1,1]{1,0:T(1,128)} %get-tuple-element.456), kind=kLoop, calls=%fused_computation.61 | loop fusion | bytes 24
  10.1 0.7 dynamic-update-slice.1
  10.8 5.1 %all-reduce.5 = (s32[4]{0:T(128)S(1)}, s32[4]{0:T(128)S(1)}, s32[4]{0:T(128)S(1)}, s32[4]{0:T(128)S(1)}, s32[4]{0:T(128)S(1)}) all-reduce(s32[4]{0:T(128)S(1)} %bitcast_dynamic-update-slice_fusion.1, s32[4]{0:T(128)S(1)} %dynamic-update-slice.1, s32[4]{0:T(128)S(1)} %subtract_dynamic-update-slice_fusion, ...), channel_id=2, replica_groups=mesh['dp'=8,'ctx'=4] {'ctx'}, use_global_device_ids=true, to_apply=%add | all-reduce | flops 20 | bytes 160 | tf_op jit(solution)/shard_map/all_gather | solution.py:16
  15.9 24.0 %while.41 = (s32[]{:T(128)}, s32[]{:T(128)}, s32[]{:T(128)}, s32[]{:T(128)}, s32[]{:T(128)}, /*index=5*/s32[4]{0:T(128)S(1)}, s32[4]{0:T(128)S(1)}, s32[4]{0:T(1...) while((s32[]{:T(128)}, s32[]{:T(128)}, s32[]{:T(128)}, s32[]{:T(128)}, ...), condition=%wide.region_3.4_spmd, body=%wide.region_2.3_spmd.sunk | while | flops 19 | bytes 375 | solution.py:25
  15.9 0.6 dynamic_slice.44
  17.0 0.6 dynamic_slice.43
  18.2 0.6 dynamic_slice.42
  19.9 0.6 dynamic_slice.41
  21.6 0.6 dynamic_slice.40
  23.9 0.6 dynamic_slice.44
  25.1 0.6 dynamic_slice.43
  26.2 0.6 dynamic_slice.42
  27.9 0.6 dynamic_slice.41
  29.7 0.6 dynamic_slice.40
  31.9 0.6 dynamic_slice.44
  33.1 0.6 dynamic_slice.43
  34.2 0.6 dynamic_slice.42
  35.9 0.6 dynamic_slice.41
  37.7 0.6 dynamic_slice.40
  40.7 0.5 multiply_cosine_fusion
  41.2 1.5 %convert_bitcast_fusion = f32[32,8,16,128]{3,1,2,0:T(8,128)S(1)} fusion(bf16[1,256,2048]{2,1,0:T(8,128)(2,1)} %param.8), kind=kLoop, calls=%fused_computation.30 | loop fusion | flops 524288 | bytes 3145728
  42.7 0.4 copy.40
  43.1 0.7 fusion.39
  43.8 1.4 %subtract_convert_fusion = (bf16[256,16,64]{2,0,1:T(8,128)(2,1)S(1)}, bf16[256,16,64]{2,0,1:T(8,128)(2,1)S(1)}) fusion(f32[256,16,64]{2,1,0:T(8,128)S(1)} %get-tuple-element.447, f32[256,16,64]{2,1,0:T(8,128)S(1)} %get-tuple-element.446, f32[256,64]{1,0:T(8,128)S(1)} %get-tuple-element.455, f32[256,64]{1,0:T(8,128)S(1)} %get-tuple-element.454), kind=kLoop, calls=%fused_computation.37 | loop fusion | flops 2097152 | bytes 3276800 | tf_op jit(solution)/shard_map/convert.3
  45.1 0.6 pad_maximum_fusion
  45.9 0.2 copy.36
  46.1 0.2 copy.37
  46.5 0.1 maximum_convert_fusion
  46.7 0.2 and_and_fusion.1
  46.9 0.8 fusion.18
  47.7 1.9 %copy-done = f32[4,256,256,4]{2,1,3,0:T(8,128)} copy-done((f32[4,256,256,4]{2,1,3,0:T(8,128)}, f32[4,256,256,4]{2,1,3,0:T(8,128)S(1)}, u32[]{:S(2)}) %copy-start) | copy-done | bytes 4194328
  49.6 1.0 %fusion.20 = f32[4,4,256]{2,1,0:T(4,128)S(1)} fusion(f32[4,256,256,4]{2,1,3,0:T(8,128)S(1)} %get-tuple-element.459, f32[4,4,256]{2,1,0:T(4,128)S(1)} %broadcast_maximum_fusion, pred[256,256]{0,1:T(8,128)(4,1)S(1)} %and_and_fusion.1), kind=kLoop, calls=%fused_computation.27 | loop fusion | flops 5238784 | bytes 4292608 | tf_op jit(solution)/shard_map/reduce_sum | solution.py:94
  50.7 5.3 %bitcast_add_fusion.1 = f32[256,4,4,128]{3,0,2,1:T(8,128)} fusion(f32[4,256,256,4]{2,1,3,0:T(8,128)} %copy-done, f32[4,4,256]{2,1,0:T(4,128)S(1)} %broadcast_maximum_fusion, pred[256,256]{0,1:T(8,128)(4,1)S(1)} %and_and_fusion.1, f32[256,4,4]{0,2,1:T(4,128)S(1)} %get-tuple-element.452, bf16[256,4,128,1]{2,1,0,3:T(4,128)(2,1)S(1)} %bitcast.152), kind=kOutput, calls=%fused_computation.29 | convolution fusion | flops 274202624 | bytes 6651904 | tf_op jit(solution)/shard_map/hgts,shd->thgd/dot_general | solution.py:95
  56.3 30.9 %while.42 = (s32[]{:T(128)}, f32[4,4,256]{2,1,0:T(4,128)S(1)}, f32[4,4,256]{2,1,0:T(4,128)S(1)}, f32[256,4,4,128]{3,0,2,1:T(8,128)}, bf16[256,512]{0,1:T(8,128)(...) while((s32[]{:T(128)}, f32[4,4,256]{2,1,0:T(4,128)S(1)}, ...), condition=%wide.region_9.10_spmd.clone, body=%wide.region_6.9_spmd.clone.sunk | while | flops 551826432 | bytes 38810448 | solution.py:164
  56.5 3.7 %collective-permute-start = (s32[256]{0:T(256)S(1)}, s32[256]{0:T(256)S(1)}, u32[]{:S(2)}, u32[]{:S(2)}) collective-permute-start(s32[256]{0:T(256)S(1)} %get-tuple-element.658), channel_id=1, source_target_pairs={{0,1},{1,2},{2,3},{4,5},{5,6},{6,7},{8,9},{9,10},{10,11},{12,13},{... | collective-permute-start | bytes 3080 | tf_op jit(solution)/shard_map/while/body/eval_jaxpr/ppermute | solution.py:31
  60.2 1.9 %collective-permute-start.1 = (bf16[256,512]{0,1:T(8,128)(2,1)S(1)}, bf16[256,512]{0,1:T(8,128)(2,1)S(1)}, u32[]{:S(2)}, u32[]{:S(2)}) collective-permute-start(bf16[256,512]{0,1:T(8,128)(2,1)S(1)} %get-tuple-element.656), channel_id=1, source_target_pairs={{0,1},{1,2},{2,3},{4,5},{5,6},{6,7},{8,9},{9,10},{10,11},{12,13},{... | collective-permute-start | bytes 786440 | tf_op jit(solution)/shard_map/while/body/eval_jaxpr/ppermute | solution.py:31
  62.1 1.9 %collective-permute-start.2 = (bf16[256,512]{0,1:T(8,128)(2,1)S(1)}, bf16[256,512]{0,1:T(8,128)(2,1)S(1)}, u32[]{:S(2)}, u32[]{:S(2)}) collective-permute-start(bf16[256,512]{0,1:T(8,128)(2,1)S(1)} %get-tuple-element.657), channel_id=1, source_target_pairs={{0,1},{1,2},{2,3},{4,5},{5,6},{6,7},{8,9},{9,10},{10,11},{12,13},{... | collective-permute-start | bytes 786440 | tf_op jit(solution)/shard_map/while/body/eval_jaxpr/ppermute | solution.py:31
  64.1 0.2 and_and_fusion.3
  64.3 1.1 %collective-permute-done.1 = bf16[256,512]{0,1:T(8,128)(2,1)S(1)} collective-permute-done((bf16[256,512]{0,1:T(8,128)(2,1)S(1)}, bf16[256,512]{0,1:T(8,128)(2,1)S(1)}, u32[]{:S(2)}, u32[]{:S(2)}) %collective-permute-start.1) | collective-permute-done | bytes 262176 | tf_op jit(solution)/shard_map/while/body/eval_jaxpr/ppermute | solution.py:31
  65.4 0.9 fusion.57
  66.3 1.0 %fusion.59 = f32[4,4,256]{2,1,0:T(4,128)S(1)} fusion(f32[4,256,256,4]{2,1,3,0:T(8,128)S(1)} %get-tuple-element.598, f32[4,4,256]{2,1,0:T(4,128)S(1)} %get-tuple-element.666, pred[256,256]{0,1:T(8,128)(4,1)S(1)} %and_and_fusion.3), kind=kLoop, calls=%fused_computation.5.clone.1 | loop fusion | flops 5238784 | bytes 4292608 | tf_op jit(solution)/shard_map/while/body/eval_jaxpr/reduce_sum | solution.py:94
  67.4 0.8 collective-permute-done.2
  68.2 1.9 %bitcast_add_fusion.3 = f32[256,4,4,128]{3,0,2,1:T(8,128)S(1)} fusion(f32[256,4,4,128]{3,0,2,1:T(8,128)S(1)} %copy-done.1, bf16[256,4,128,1]{0,2,3,1:T(8,128)(2,1)S(1)} %bitcast.143, f32[4,256,256,4]{2,1,3,0:T(8,128)S(1)} %get-tuple-element.598, f32[4,4,256]{2,1,0:T(4,128)S(1)} %get-tuple-element.666, pred[256,256]{0,1:T(8,128)(4,1)S(1)} %and_and_fusion.3, ...), kind=kOutput, calls=%fused_computation.7.clone.1 | convolution fusion | flops 274726912 | bytes 8749056 | tf_op jit(solution)/shard_map/while/body/eval_jaxpr/hgts,shd->thgd/dot_general | solution.py:95
  70.2 1.3 %copy-done.2 = f32[256,4,4,128]{3,0,2,1:T(8,128)} copy-done((f32[256,4,4,128]{3,0,2,1:T(8,128)}, f32[256,4,4,128]{3,0,2,1:T(8,128)S(1)}, u32[]{:S(2)}) %copy-start.2) | copy-done | bytes 2097176 | tf_op jit(solution)/shard_map/while
  71.5 4.4 %collective-permute-start = (s32[256]{0:T(256)S(1)}, s32[256]{0:T(256)S(1)}, u32[]{:S(2)}, u32[]{:S(2)}) collective-permute-start(s32[256]{0:T(256)S(1)} %get-tuple-element.658), channel_id=1, source_target_pairs={{0,1},{1,2},{2,3},{4,5},{5,6},{6,7},{8,9},{9,10},{10,11},{12,13},{... | collective-permute-start | bytes 3080 | tf_op jit(solution)/shard_map/while/body/eval_jaxpr/ppermute | solution.py:31
  75.9 1.9 %collective-permute-start.1 = (bf16[256,512]{0,1:T(8,128)(2,1)S(1)}, bf16[256,512]{0,1:T(8,128)(2,1)S(1)}, u32[]{:S(2)}, u32[]{:S(2)}) collective-permute-start(bf16[256,512]{0,1:T(8,128)(2,1)S(1)} %get-tuple-element.656), channel_id=1, source_target_pairs={{0,1},{1,2},{2,3},{4,5},{5,6},{6,7},{8,9},{9,10},{10,11},{12,13},{... | collective-permute-start | bytes 786440 | tf_op jit(solution)/shard_map/while/body/eval_jaxpr/ppermute | solution.py:31
  77.8 1.9 %collective-permute-start.2 = (bf16[256,512]{0,1:T(8,128)(2,1)S(1)}, bf16[256,512]{0,1:T(8,128)(2,1)S(1)}, u32[]{:S(2)}, u32[]{:S(2)}) collective-permute-start(bf16[256,512]{0,1:T(8,128)(2,1)S(1)} %get-tuple-element.657), channel_id=1, source_target_pairs={{0,1},{1,2},{2,3},{4,5},{5,6},{6,7},{8,9},{9,10},{10,11},{12,13},{... | collective-permute-start | bytes 786440 | tf_op jit(solution)/shard_map/while/body/eval_jaxpr/ppermute | solution.py:31
  79.8 0.2 and_and_fusion.3
  80.0 1.1 %collective-permute-done.1 = bf16[256,512]{0,1:T(8,128)(2,1)S(1)} collective-permute-done((bf16[256,512]{0,1:T(8,128)(2,1)S(1)}, bf16[256,512]{0,1:T(8,128)(2,1)S(1)}, u32[]{:S(2)}, u32[]{:S(2)}) %collective-permute-start.1) | collective-permute-done | bytes 262176 | tf_op jit(solution)/shard_map/while/body/eval_jaxpr/ppermute | solution.py:31
  81.1 0.9 fusion.57
  82.0 1.0 %fusion.59 = f32[4,4,256]{2,1,0:T(4,128)S(1)} fusion(f32[4,256,256,4]{2,1,3,0:T(8,128)S(1)} %get-tuple-element.598, f32[4,4,256]{2,1,0:T(4,128)S(1)} %get-tuple-element.666, pred[256,256]{0,1:T(8,128)(4,1)S(1)} %and_and_fusion.3), kind=kLoop, calls=%fused_computation.5.clone.1 | loop fusion | flops 5238784 | bytes 4292608 | tf_op jit(solution)/shard_map/while/body/eval_jaxpr/reduce_sum | solution.py:94
  83.1 0.8 collective-permute-done.2
  83.9 1.9 %bitcast_add_fusion.3 = f32[256,4,4,128]{3,0,2,1:T(8,128)S(1)} fusion(f32[256,4,4,128]{3,0,2,1:T(8,128)S(1)} %copy-done.1, bf16[256,4,128,1]{0,2,3,1:T(8,128)(2,1)S(1)} %bitcast.143, f32[4,256,256,4]{2,1,3,0:T(8,128)S(1)} %get-tuple-element.598, f32[4,4,256]{2,1,0:T(4,128)S(1)} %get-tuple-element.666, pred[256,256]{0,1:T(8,128)(4,1)S(1)} %and_and_fusion.3, ...), kind=kOutput, calls=%fused_computation.7.clone.1 | convolution fusion | flops 274726912 | bytes 8749056 | tf_op jit(solution)/shard_map/while/body/eval_jaxpr/hgts,shd->thgd/dot_general | solution.py:95
  85.9 1.3 %copy-done.2 = f32[256,4,4,128]{3,0,2,1:T(8,128)} copy-done((f32[256,4,4,128]{3,0,2,1:T(8,128)}, f32[256,4,4,128]{3,0,2,1:T(8,128)S(1)}, u32[]{:S(2)}) %copy-start.2) | copy-done | bytes 2097176 | tf_op jit(solution)/shard_map/while
  87.2 1.9 %divide_convert_fusion = bf16[256,4,4,128]{3,0,2,1:T(8,128)(2,1)S(1)} fusion(f32[256,4,4,128]{3,0,2,1:T(8,128)} %get-tuple-element.364, f32[256,4,4]{0,2,1:T(4,128)S(1)} %bitcast.149), kind=kLoop, calls=%fused_computation.31 | loop fusion | flops 1048576 | bytes 3162112 | tf_op jit(solution)/shard_map/convert_element_type | solution.py:169
  89.1 0.8 copy.23
  89.9 1.6 %convert_element_type.68 = bf16[1,256,2048]{2,1,0:T(8,128)(2,1)} reshape(bf16[256,4,4,128]{3,2,1,0:T(4,128)(2,1)S(1)} %copy.23) | data formatting | bytes 2097152 | tf_op jit(solution)/shard_map/convert_element_type | solution.py:169
  (53 shorter events, 1.2 us)
Async XLA Ops:
  43.7 2.0 %copy-start.4 = (bf16[1,256,512]{2,1,0:T(8,128)(2,1)S(1)}, bf16[1,256,512]{2,1,0:T(8,128)(2,1)}, u32[]{:S(2)}) copy-start(bf16[1,256,512]{2,1,0:T(8,128)(2,1)} %param.9) | copy-start | bytes 786436
  45.1 1.5 %copy-start.5 = (s32[1,256]{1,0:T(1,128)S(1)}, s32[1,256]{1,0:T(1,128)}, u32[]{:S(2)}) copy-start(s32[1,256]{1,0:T(1,128)} %param.11) | copy-start | bytes 3076
  46.8 3.8 %copy-start.3 = (bf16[1,256,512]{2,1,0:T(8,128)(2,1)S(1)}, bf16[1,256,512]{2,1,0:T(8,128)(2,1)}, u32[]{:S(2)}) copy-start(bf16[1,256,512]{2,1,0:T(8,128)(2,1)} %param.10) | copy-start | bytes 786436
  47.6 1.9 %copy-start = (f32[4,256,256,4]{2,1,3,0:T(8,128)}, f32[4,256,256,4]{2,1,3,0:T(8,128)S(1)}, u32[]{:S(2)}) copy-start(f32[4,256,256,4]{2,1,3,0:T(8,128)S(1)} %get-tuple-element.459) | copy-start | bytes 12582916
  56.5 7.6 %collective-permute-start = (s32[256]{0:T(256)S(1)}, s32[256]{0:T(256)S(1)}, u32[]{:S(2)}, u32[]{:S(2)}) collective-permute-start(s32[256]{0:T(256)S(1)} %get-tuple-element.658), channel_id=1, source_target_pairs={{0,1},{1,2},{2,3},{4,5},{5,6},{6,7},{8,9},{9,10},{10,11},{12,13},{... | collective-permute-start | bytes 3080 | tf_op jit(solution)/shard_map/while/body/eval_jaxpr/ppermute | solution.py:31
  60.2 5.2 %collective-permute-start.1 = (bf16[256,512]{0,1:T(8,128)(2,1)S(1)}, bf16[256,512]{0,1:T(8,128)(2,1)S(1)}, u32[]{:S(2)}, u32[]{:S(2)}) collective-permute-start(bf16[256,512]{0,1:T(8,128)(2,1)S(1)} %get-tuple-element.656), channel_id=1, source_target_pairs={{0,1},{1,2},{2,3},{4,5},{5,6},{6,7},{8,9},{9,10},{10,11},{12,13},{... | collective-permute-start | bytes 786440 | tf_op jit(solution)/shard_map/while/body/eval_jaxpr/ppermute | solution.py:31
  62.1 6.1 %collective-permute-start.2 = (bf16[256,512]{0,1:T(8,128)(2,1)S(1)}, bf16[256,512]{0,1:T(8,128)(2,1)S(1)}, u32[]{:S(2)}, u32[]{:S(2)}) collective-permute-start(bf16[256,512]{0,1:T(8,128)(2,1)S(1)} %get-tuple-element.657), channel_id=1, source_target_pairs={{0,1},{1,2},{2,3},{4,5},{5,6},{6,7},{8,9},{9,10},{10,11},{12,13},{... | collective-permute-start | bytes 786440 | tf_op jit(solution)/shard_map/while/body/eval_jaxpr/ppermute | solution.py:31
  65.4 2.8 %copy-start.1 = (f32[256,4,4,128]{3,0,2,1:T(8,128)S(1)}, f32[256,4,4,128]{3,0,2,1:T(8,128)}, u32[]{:S(2)}) copy-start(f32[256,4,4,128]{3,0,2,1:T(8,128)} %get-tuple-element.655) | copy-start | bytes 6291460 | tf_op jit(solution)/shard_map/while
  70.2 1.3 %copy-start.2 = (f32[256,4,4,128]{3,0,2,1:T(8,128)}, f32[256,4,4,128]{3,0,2,1:T(8,128)S(1)}, u32[]{:S(2)}) copy-start(f32[256,4,4,128]{3,0,2,1:T(8,128)S(1)} %bitcast_add_fusion.3) | copy-start | bytes 6291460 | tf_op jit(solution)/shard_map/while
  71.5 8.3 %collective-permute-start = (s32[256]{0:T(256)S(1)}, s32[256]{0:T(256)S(1)}, u32[]{:S(2)}, u32[]{:S(2)}) collective-permute-start(s32[256]{0:T(256)S(1)} %get-tuple-element.658), channel_id=1, source_target_pairs={{0,1},{1,2},{2,3},{4,5},{5,6},{6,7},{8,9},{9,10},{10,11},{12,13},{... | collective-permute-start | bytes 3080 | tf_op jit(solution)/shard_map/while/body/eval_jaxpr/ppermute | solution.py:31
  75.9 5.2 %collective-permute-start.1 = (bf16[256,512]{0,1:T(8,128)(2,1)S(1)}, bf16[256,512]{0,1:T(8,128)(2,1)S(1)}, u32[]{:S(2)}, u32[]{:S(2)}) collective-permute-start(bf16[256,512]{0,1:T(8,128)(2,1)S(1)} %get-tuple-element.656), channel_id=1, source_target_pairs={{0,1},{1,2},{2,3},{4,5},{5,6},{6,7},{8,9},{9,10},{10,11},{12,13},{... | collective-permute-start | bytes 786440 | tf_op jit(solution)/shard_map/while/body/eval_jaxpr/ppermute | solution.py:31
  77.8 6.1 %collective-permute-start.2 = (bf16[256,512]{0,1:T(8,128)(2,1)S(1)}, bf16[256,512]{0,1:T(8,128)(2,1)S(1)}, u32[]{:S(2)}, u32[]{:S(2)}) collective-permute-start(bf16[256,512]{0,1:T(8,128)(2,1)S(1)} %get-tuple-element.657), channel_id=1, source_target_pairs={{0,1},{1,2},{2,3},{4,5},{5,6},{6,7},{8,9},{9,10},{10,11},{12,13},{... | collective-permute-start | bytes 786440 | tf_op jit(solution)/shard_map/while/body/eval_jaxpr/ppermute | solution.py:31
  81.1 2.8 %copy-start.1 = (f32[256,4,4,128]{3,0,2,1:T(8,128)S(1)}, f32[256,4,4,128]{3,0,2,1:T(8,128)}, u32[]{:S(2)}) copy-start(f32[256,4,4,128]{3,0,2,1:T(8,128)} %get-tuple-element.655) | copy-start | bytes 6291460 | tf_op jit(solution)/shard_map/while
  85.8 1.3 %copy-start.2 = (f32[256,4,4,128]{3,0,2,1:T(8,128)}, f32[256,4,4,128]{3,0,2,1:T(8,128)S(1)}, u32[]{:S(2)}) copy-start(f32[256,4,4,128]{3,0,2,1:T(8,128)S(1)} %bitcast_add_fusion.3) | copy-start | bytes 6291460 | tf_op jit(solution)/shard_map/while
where the time goes:
time: 92.2 us; the launch traced here: 91.6 us
  local copies, waits for them, and re-layouts  24.4 us (26%)
  loops' own time  15.8 us (17%)
  starting transfers between devices  15.8 us (17%)
  other arithmetic  12 us (13%)
  matrix products  11.7 us (13%)
  blocking collectives  5.07 us (5%)
  waiting for transfers between devices  3.95 us (4%)
  between operations  2.94 us (3%)
    ppermute x6, starting transfers between devices, from_behind(): return lax.ppermute(block, axis, route)  15.8 us
    another operation x1, loops' own time, entering(): return lax.fori_loop(0, count - 1, hop, running)  15.3 us
    dot_general x3, matrix products, attend_piece(): jnp.einsum('hgts,shd->thgd', weights.astype(jnp.bfloat16), value_heads, p...  9.11 us
    dynamic_slice x15, local copies, waits for them, and re-layouts, hop(): longer = join(running, jax.tree.map(lambda part: part[position], pieces))  8.71 us
    unnamed x24, local copies, waits for them, and re-layouts  8.3 us
    all_gather x1, blocking collectives, entering(): pieces = jax.tree.map(lambda part: lax.all_gather(part, axis), value)  5.07 us
    ppermute x6, waiting for transfers between devices, from_behind(): return lax.ppermute(block, axis, route)  3.95 us
    reduce_sum x3, other arithmetic, attend_piece(): new_sum = run_sum * rescale + jnp.sum(weights, axis=-1)  3.11 us
  transfers between devices with their start and end apart: 6, of which 4 were waited for; matrix products, arithmetic and copies ran while one was open for 5% of the time, Pallas kernels for 0%

commit v1 on v0

v1 whole, which is shorter than its diff:
```python
import functools
import math

import jax
import jax.numpy as jnp
import numpy as np
from jax import lax
from jax.experimental import pallas as pl
from jax.experimental.pallas import tpu as pltpu
from jax.sharding import PartitionSpec as P

HQ = 16
HK = 4
HD = 128
GROUP = HQ // HK
ROPE_THETA = 500000.0
LANES = 128
DEAD = -1e30


def frequencies():
    half = HD // 2
    steps = np.arange(half, dtype=np.float32)
    log_theta = np.log(np.float32(ROPE_THETA))
    freq = np.exp(-log_theta * np.float32(2.0) * steps / np.float32(HD)).astype(np.float32)
    return np.concatenate([freq, freq])[None, :]


def turn_cos(turns):
    square = turns * turns
    total = jnp.full_like(square, COS_TERMS[-1])
    for term in COS_TERMS[-2::-1]:
        total = total * square + term
    return total


COS_TERMS = [
    (-1.0) ** n * (2.0 * math.pi) ** (2 * n) / math.factorial(2 * n) for n in range(11)
]
TURN = 2.0 * math.pi
TURN_HIGH = 6.28125
TURN_MID = float(np.float32(np.round((TURN - TURN_HIGH) * 2**22) / 2**22))
TURN_LOW = TURN - TURN_HIGH - TURN_MID


def cos_and_sin(positions, freq):
    angle = positions * freq
    whole = jnp.round(angle * (1.0 / TURN))
    rest = ((angle - whole * TURN_HIGH) - whole * TURN_MID) - whole * TURN_LOW
    turns = rest * (1.0 / TURN)
    lane = lax.broadcasted_iota(jnp.int32, turns.shape, 1)
    turns = jnp.where(lane < HD // 2, turns, turns - 0.25)
    turns = turns - jnp.round(turns)
    return turn_cos(turns)


def rope_factors(positions, freq):
    both = cos_and_sin(positions, freq)
    swapped = pltpu.roll(both, HD // 2, 1)
    lane = lax.broadcasted_iota(jnp.int32, both.shape, 1)
    low = lane < HD // 2
    return jnp.where(low, both, swapped), jnp.where(low, -swapped, both)


def turned(rows, cosine, sine):
    wide = rows.astype(jnp.float32)
    return (wide * cosine + pltpu.roll(wide, HD // 2, 1) * sine).astype(jnp.bfloat16)


def columns_of(row, width):
    pieces = []
    for at in range(0, width, LANES):
        size = min(LANES, width - at)
        eye = lax.broadcasted_iota(jnp.int32, (size, size), 0) == lax.broadcasted_iota(
            jnp.int32, (size, size), 1
        )
        pieces.append(
            jnp.sum(jnp.where(eye, row[:, at : at + size], 0.0), axis=1, keepdims=True)
        )
    return jnp.concatenate(pieces, axis=0)


def attend(hops, rows, mine_ref, freq_ref, *refs):
    blocks = hops + 1
    window = blocks * rows
    seg_refs = refs[:blocks]
    key_refs = refs[blocks : 2 * blocks]
    value_refs = refs[2 * blocks : 3 * blocks]
    query_ref, out_ref, cos_ref, sin_ref, bias_ref = refs[3 * blocks :]

    @pl.when(pl.program_id(0) == 0)
    def prepare():
        mine = mine_ref[0]
        parts = []
        for at in range(blocks):
            back = hops - at
            part = seg_refs[at][...].astype(jnp.float32)
            parts.append(jnp.where(mine >= back, part, -1.0))
        row = jnp.concatenate(parts, axis=1)
        column = columns_of(row, window)
        first = jnp.sum((row < column).astype(jnp.float32), axis=1, keepdims=True)
        place = lax.broadcasted_iota(jnp.int32, (window, 1), 0).astype(jnp.float32)
        cosine, sine = rope_factors(place - first, freq_ref[...])
        cos_ref[...] = cosine
        sin_ref[...] = sine
        key_place = lax.broadcasted_iota(jnp.int32, (rows, window), 1).astype(jnp.float32)
        live = (key_place >= first[hops * rows :]) & (key_place <= place[hops * rows :])
        bias_ref[...] = jnp.where(live, 0.0, DEAD)

    own = pl.ds(hops * rows, rows)
    rot_q = jnp.concatenate(
        [
            turned(query_ref[:, g * HD : (g + 1) * HD], cos_ref[own, :], sin_ref[own, :])
            for g in range(GROUP)
        ],
        axis=0,
    )
    rot_k = jnp.concatenate(
        [
            turned(
                key_refs[at][...],
                cos_ref[at * rows : (at + 1) * rows, :],
                sin_ref[at * rows : (at + 1) * rows, :],
            )
            for at in range(blocks)
        ],
        axis=0,
    )
    scores = lax.dot_general(
        rot_q, rot_k, (((1,), (1,)), ((), ())), preferred_element_type=jnp.float32
    )
    scores = scores.reshape(GROUP, rows, window) + bias_ref[...][None]
    scores = scores.reshape(GROUP * rows, window)
    top = jnp.max(scores, axis=1, keepdims=True)
    weights = jnp.exp2((scores - top) * (math.log2(math.e) / math.sqrt(HD)))
    denom = jnp.sum(weights, axis=1, keepdims=True)
    values = jnp.concatenate([ref[...] for ref in value_refs], axis=0)
    total = jnp.dot(weights.astype(jnp.bfloat16), values, preferred_element_type=jnp.float32)
    result = (total * (1.0 / denom)).astype(jnp.bfloat16)
    for g in range(GROUP):
        out_ref[:, g * HD : (g + 1) * HD] = result[g * rows : (g + 1) * rows]


def body(queries, keys, values, segments):
    rows = segments.shape[1]
    size = lax.axis_size("ctx")
    hops = size // 2
    mine = lax.axis_index("ctx").astype(jnp.int32).reshape(1)

    def behind(block, distance):
        return lax.ppermute(
            block, "ctx", [(i, i + distance) for i in range(size - distance)]
        )

    distances = list(range(hops, 0, -1))
    seg_blocks = [behind(segments, d) for d in distances] + [segments]
    key_blocks = [behind(keys[0], d) for d in distances] + [keys[0]]
    value_blocks = [behind(values[0], d) for d in distances] + [values[0]]
    blocks = hops + 1
    window = blocks * rows
    whole = pl.BlockSpec((1, rows), lambda h: (0, 0))
    head = pl.BlockSpec((rows, HD), lambda h: (0, h))
    group = pl.BlockSpec((rows, GROUP * HD), lambda h: (0, h))
    out = pl.pallas_call(
        functools.partial(attend, hops, rows),
        grid=(HK,),
        out_shape=jax.ShapeDtypeStruct((rows, HQ * HD), jnp.bfloat16),
        in_specs=[
            pl.BlockSpec(memory_space=pltpu.SMEM),
            pl.BlockSpec((1, HD), lambda h: (0, 0)),
        ]
        + [whole] * blocks
        + [head] * (2 * blocks)
        + [group],
        out_specs=group,
        scratch_shapes=[
            pltpu.VMEM((window, HD), jnp.float32),
            pltpu.VMEM((window, HD), jnp.float32),
            pltpu.VMEM((rows, window), jnp.float32),
        ],
        compiler_params=pltpu.CompilerParams(vmem_limit_bytes=48 << 20),
        name="attend",
    )(mine, jnp.asarray(frequencies()), *seg_blocks, *key_blocks, *value_blocks, queries[0])
    return out[None]


def solution(mesh):
    placed = (P("dp", "ctx", None), P("dp", "ctx", None), P("dp", "ctx", None), P("dp", "ctx"))
    return jax.shard_map(
        body, mesh=mesh, in_specs=placed, out_specs=P("dp", "ctx", None), check_vma=False
    )
```

time: 92.2 us -> 40.5 us (0.44)
  the two profiles are of different devices: /device:TPU:1 before, /device:TPU:21 now
where the time goes in v1:
time: 40.5 us; the launch traced here: 39.8 us
  waiting for transfers between devices  17.2 us (42%)
  Pallas kernels  10.8 us (27%)
  starting transfers between devices  7.86 us (19%)
  local copies, waits for them, and re-layouts  3.78 us (9%)
    ppermute x6, waiting for transfers between devices, behind(): lax.ppermute(block, 'ctx', [(i, i + distance) for i in range(size - dista...  17.2 us
    pallas_call x1, Pallas kernels, body(): pl.pallas_call(functools.partial(attend, hops, rows), grid=(HK,), out_sha...  10.8 us
    ppermute x6, starting transfers between devices, behind(): lax.ppermute(block, 'ctx', [(i, i + distance) for i in range(size - dista...  7.86 us
    unnamed x10, local copies, waits for them, and re-layouts  3.78 us
  transfers between devices with their start and end apart: 6, of which 2 were waited for; matrix products, arithmetic and copies ran while one was open for 0% of the time, Pallas kernels for 0%

profile of v1, /device:TPU:21, one launch (start us, length us, event | category | flops | bytes accessed | tf_op | source)
XLA Modules:
  0.0 39.8 jit_solution(12358946659723396027)
XLA Ops:
  0.0 0.0 copy-start.3
  0.0 1.4 %collective-permute-start.3 = (bf16[256,512]{1,0:T(8,128)(2,1)}, bf16[256,512]{1,0:T(8,128)(2,1)S(1)}, u32[]{:S(2)}, u32[]{:S(2)}) collective-permute-start(bf16[256,512]{1,0:T(8,128)(2,1)} %bitcast.6), channel_id=1, source_target_pairs={{0,1},{1,2},{2,3},{4,5},{5,6},{6,7},{8,9},{9,10},{10,11},{12,13},{... | collective-permute-start | bytes 786440 | tf_op jit(solution)/shard_map/ppermute | solution.py:151
  1.4 1.3 %collective-permute-start.2 = (bf16[256,512]{1,0:T(8,128)(2,1)}, bf16[256,512]{1,0:T(8,128)(2,1)S(1)}, u32[]{:S(2)}, u32[]{:S(2)}) collective-permute-start(bf16[256,512]{1,0:T(8,128)(2,1)} %bitcast.7), channel_id=1, source_target_pairs={{0,2},{1,3},{4,6},{5,7},{8,10},{9,11},{12,14},{13,15},{16,18},{17,... | collective-permute-start | bytes 786440 | tf_op jit(solution)/shard_map/ppermute | solution.py:151
  2.7 1.3 %collective-permute-start.5 = (bf16[256,512]{1,0:T(8,128)(2,1)}, bf16[256,512]{1,0:T(8,128)(2,1)S(1)}, u32[]{:S(2)}, u32[]{:S(2)}) collective-permute-start(bf16[256,512]{1,0:T(8,128)(2,1)} %bitcast.9), channel_id=1, source_target_pairs={{0,1},{1,2},{2,3},{4,5},{5,6},{6,7},{8,9},{9,10},{10,11},{12,13},{... | collective-permute-start | bytes 786440 | tf_op jit(solution)/shard_map/ppermute | solution.py:151
  4.0 1.3 %collective-permute-start.4 = (bf16[256,512]{1,0:T(8,128)(2,1)}, bf16[256,512]{1,0:T(8,128)(2,1)S(1)}, u32[]{:S(2)}, u32[]{:S(2)}) collective-permute-start(bf16[256,512]{1,0:T(8,128)(2,1)} %bitcast.10), channel_id=1, source_target_pairs={{0,2},{1,3},{4,6},{5,7},{8,10},{9,11},{12,14},{13,15},{16,18},{17,... | collective-permute-start | bytes 786440 | tf_op jit(solution)/shard_map/ppermute | solution.py:151
  5.3 0.0 copy-done.3
  5.3 1.3 %collective-permute-start = (s32[1,256]{1,0:T(1,128)S(1)}, s32[1,256]{1,0:T(1,128)S(1)}, u32[]{:S(2)}, u32[]{:S(2)}) collective-permute-start(s32[1,256]{1,0:T(1,128)S(1)} %copy-done.3), channel_id=1, source_target_pairs={{0,2},{1,3},{4,6},{5,7},{8,10},{9,11},{12,14},{13,15},{16,18},{17,... | collective-permute-start | bytes 3080 | tf_op jit(solution)/shard_map/ppermute | solution.py:151
  6.6 15.5 %collective-permute-done.refs_0_ = s32[1,256]{1,0:T(1,128)S(1)} collective-permute-done((s32[1,256]{1,0:T(1,128)S(1)}, s32[1,256]{1,0:T(1,128)S(1)}, u32[]{:S(2)}, u32[]{:S(2)}) %collective-permute-start) | collective-permute-done | bytes 1056 | tf_op jit(solution)/shard_map/ppermute | solution.py:151
  22.1 1.3 %collective-permute-start.1 = (s32[1,256]{1,0:T(1,128)S(1)}, s32[1,256]{1,0:T(1,128)S(1)}, u32[]{:S(2)}, u32[]{:S(2)}) collective-permute-start(s32[1,256]{1,0:T(1,128)S(1)} %copy-done.3), channel_id=1, source_target_pairs={{0,1},{1,2},{2,3},{4,5},{5,6},{6,7},{8,9},{9,10},{10,11},{12,13},{... | collective-permute-start | bytes 3080 | tf_op jit(solution)/shard_map/ppermute | solution.py:151
  23.4 1.8 %collective-permute-done.1.refs_1_ = s32[1,256]{1,0:T(1,128)S(1)} collective-permute-done((s32[1,256]{1,0:T(1,128)S(1)}, s32[1,256]{1,0:T(1,128)S(1)}, u32[]{:S(2)}, u32[]{:S(2)}) %collective-permute-start.1) | collective-permute-done | bytes 1056 | tf_op jit(solution)/shard_map/ppermute | solution.py:151
  25.2 0.0 collective-permute-done.3.refs_4_
  25.2 0.0 collective-permute-done.2.refs_3_
  25.2 0.0 collective-permute-done.5.refs_7_
  25.2 0.0 collective-permute-done.4.refs_6_
  25.2 0.0 copy-start.4
  25.2 0.6 %copy-done.4 = f32[1,128]{1,0:T(1,128)S(1)} copy-done((f32[1,128]{1,0:T(1,128)S(1)}, f32[1,128]{1,0:T(1,128)}, u32[]{:S(2)}) %copy-start.4) | copy-done | bytes 536
  25.8 0.0 copy-start
  25.8 1.2 %copy-done = bf16[1,256,2048]{2,1,0:T(8,128)(2,1)S(1)} copy-done((bf16[1,256,2048]{2,1,0:T(8,128)(2,1)S(1)}, bf16[1,256,2048]{2,1,0:T(8,128)(2,1)}, u32[]{:S(2)}) %copy-start) | copy-done | bytes 1048600
  27.1 0.0 copy-start.1
  27.1 0.9 %copy-done.1 = bf16[1,256,512]{2,1,0:T(8,128)(2,1)S(1)} copy-done((bf16[1,256,512]{2,1,0:T(8,128)(2,1)S(1)}, bf16[1,256,512]{2,1,0:T(8,128)(2,1)}, u32[]{:S(2)}) %copy-start.1) | copy-done | bytes 262168
  28.0 0.0 copy-start.2
  28.0 0.9 %copy-done.2 = bf16[1,256,512]{2,1,0:T(8,128)(2,1)S(1)} copy-done((bf16[1,256,512]{2,1,0:T(8,128)(2,1)S(1)}, bf16[1,256,512]{2,1,0:T(8,128)(2,1)}, u32[]{:S(2)}) %copy-start.2) | copy-done | bytes 262168
  29.0 10.8 %attend.1 = bf16[256,2048]{1,0:T(8,128)(2,1)} custom-call(s32[1]{0:T(128)} %bitcast.mine_ref, f32[1,128]{1,0:T(1,128)S(1)} %copy-done.4, s32[1,256]{1,0:T(1,128)S(1)} %collective-permute-done.refs_0_, s32[1,256]{1,0:T(1,128)S(1)} %collective-permute-done.1.refs_1_, s32[1,256]{1,0:T(1,128)S(1)} %copy-done.3, ...), custom_call_target="tpu_custom_call" | custom-call | tf_op jit(solution)/shard_map/attend/pallas_call | solution.py:164
Async XLA Ops:
  0.0 5.3 %copy-start.3 = (s32[1,256]{1,0:T(1,128)S(1)}, s32[1,256]{1,0:T(1,128)}, u32[]{:S(2)}) copy-start(s32[1,256]{1,0:T(1,128)} %refs_2_.1) | copy-start | bytes 3076
  0.0 25.2 %collective-permute-start.3 = (bf16[256,512]{1,0:T(8,128)(2,1)}, bf16[256,512]{1,0:T(8,128)(2,1)S(1)}, u32[]{:S(2)}, u32[]{:S(2)}) collective-permute-start(bf16[256,512]{1,0:T(8,128)(2,1)} %bitcast.6), channel_id=1, source_target_pairs={{0,1},{1,2},{2,3},{4,5},{5,6},{6,7},{8,9},{9,10},{10,11},{12,13},{... | collective-permute-start | bytes 786440 | tf_op jit(solution)/shard_map/ppermute | solution.py:151
  1.4 23.7 %collective-permute-start.2 = (bf16[256,512]{1,0:T(8,128)(2,1)}, bf16[256,512]{1,0:T(8,128)(2,1)S(1)}, u32[]{:S(2)}, u32[]{:S(2)}) collective-permute-start(bf16[256,512]{1,0:T(8,128)(2,1)} %bitcast.7), channel_id=1, source_target_pairs={{0,2},{1,3},{4,6},{5,7},{8,10},{9,11},{12,14},{13,15},{16,18},{17,... | collective-permute-start | bytes 786440 | tf_op jit(solution)/shard_map/ppermute | solution.py:151
  2.7 22.4 %collective-permute-start.5 = (bf16[256,512]{1,0:T(8,128)(2,1)}, bf16[256,512]{1,0:T(8,128)(2,1)S(1)}, u32[]{:S(2)}, u32[]{:S(2)}) collective-permute-start(bf16[256,512]{1,0:T(8,128)(2,1)} %bitcast.9), channel_id=1, source_target_pairs={{0,1},{1,2},{2,3},{4,5},{5,6},{6,7},{8,9},{9,10},{10,11},{12,13},{... | collective-permute-start | bytes 786440 | tf_op jit(solution)/shard_map/ppermute | solution.py:151
  4.0 21.2 %collective-permute-start.4 = (bf16[256,512]{1,0:T(8,128)(2,1)}, bf16[256,512]{1,0:T(8,128)(2,1)S(1)}, u32[]{:S(2)}, u32[]{:S(2)}) collective-permute-start(bf16[256,512]{1,0:T(8,128)(2,1)} %bitcast.10), channel_id=1, source_target_pairs={{0,2},{1,3},{4,6},{5,7},{8,10},{9,11},{12,14},{13,15},{16,18},{17,... | collective-permute-start | bytes 786440 | tf_op jit(solution)/shard_map/ppermute | solution.py:151
  5.3 16.8 %collective-permute-start = (s32[1,256]{1,0:T(1,128)S(1)}, s32[1,256]{1,0:T(1,128)S(1)}, u32[]{:S(2)}, u32[]{:S(2)}) collective-permute-start(s32[1,256]{1,0:T(1,128)S(1)} %copy-done.3), channel_id=1, source_target_pairs={{0,2},{1,3},{4,6},{5,7},{8,10},{9,11},{12,14},{13,15},{16,18},{17,... | collective-permute-start | bytes 3080 | tf_op jit(solution)/shard_map/ppermute | solution.py:151
  22.1 3.0 %collective-permute-start.1 = (s32[1,256]{1,0:T(1,128)S(1)}, s32[1,256]{1,0:T(1,128)S(1)}, u32[]{:S(2)}, u32[]{:S(2)}) collective-permute-start(s32[1,256]{1,0:T(1,128)S(1)} %copy-done.3), channel_id=1, source_target_pairs={{0,1},{1,2},{2,3},{4,5},{5,6},{6,7},{8,9},{9,10},{10,11},{12,13},{... | collective-permute-start | bytes 3080 | tf_op jit(solution)/shard_map/ppermute | solution.py:151
  25.2 0.7 %copy-start.4 = (f32[1,128]{1,0:T(1,128)S(1)}, f32[1,128]{1,0:T(1,128)}, u32[]{:S(2)}) copy-start(f32[1,128]{1,0:T(1,128)} %constant.6.clone.freq_ref) | copy-start | bytes 1540
  25.8 1.2 %copy-start = (bf16[1,256,2048]{2,1,0:T(8,128)(2,1)S(1)}, bf16[1,256,2048]{2,1,0:T(8,128)(2,1)}, u32[]{:S(2)}) copy-start(bf16[1,256,2048]{2,1,0:T(8,128)(2,1)} %param.5) | copy-start | bytes 3145732
  27.1 0.9 %copy-start.1 = (bf16[1,256,512]{2,1,0:T(8,128)(2,1)S(1)}, bf16[1,256,512]{2,1,0:T(8,128)(2,1)}, u32[]{:S(2)}) copy-start(bf16[1,256,512]{2,1,0:T(8,128)(2,1)} %param.6) | copy-start | bytes 786436
  28.0 0.9 %copy-start.2 = (bf16[1,256,512]{2,1,0:T(8,128)(2,1)S(1)}, bf16[1,256,512]{2,1,0:T(8,128)(2,1)}, u32[]{:S(2)}) copy-start(bf16[1,256,512]{2,1,0:T(8,128)(2,1)} %param.7) | copy-start | bytes 786436

commit v2 on v1

v2 whole, which is shorter than its diff:
```python
import functools
import math

import jax
import jax.numpy as jnp
import numpy as np
from jax import lax
from jax.experimental import pallas as pl
from jax.experimental.pallas import tpu as pltpu
from jax.sharding import PartitionSpec as P

HQ = 16
HK = 4
HD = 128
GROUP = HQ // HK
ROPE_THETA = 500000.0
LANES = 128
DEAD = -1e30


def frequencies():
    half = HD // 2
    steps = np.arange(half, dtype=np.float32)
    log_theta = np.log(np.float32(ROPE_THETA))
    freq = np.exp(-log_theta * np.float32(2.0) * steps / np.float32(HD)).astype(np.float32)
    return np.concatenate([freq, freq])[None, :]


TURN = 2.0 * math.pi
TURN_HIGH = 6.28125
TURN_MID = float(np.float32(np.round((TURN - TURN_HIGH) * 2**22) / 2**22))
TURN_LOW = TURN - TURN_HIGH - TURN_MID
SIN_TERMS = [(-1.0) ** n * TURN ** (2 * n + 1) / math.factorial(2 * n + 1) for n in range(7)]
SCALE = math.log2(math.e) / math.sqrt(HD)
TILE = 128


def rope_factors(positions, freq):
    angle = positions * freq
    whole = jnp.round(angle * (1.0 / TURN))
    rest = ((angle - whole * TURN_HIGH) - whole * TURN_MID) - whole * TURN_LOW
    turns = rest * (1.0 / TURN)
    lane = lax.broadcasted_iota(jnp.int32, freq.shape, 1)
    low = lane < HD // 2
    turns = turns - jnp.where(low, 0.0, 0.25)
    turns = turns - jnp.round(turns)
    part = 0.25 - jnp.abs(turns)
    square = part * part
    total = jnp.full_like(square, SIN_TERMS[-1])
    for term in SIN_TERMS[-2::-1]:
        total = total * square + term
    both = total * part
    swapped = pltpu.roll(both, HD // 2, 1)
    return jnp.where(low, both, swapped), jnp.where(low, -swapped, both)


def turned(rows, cosine, sine):
    wide = rows.astype(jnp.float32)
    return (wide * cosine + pltpu.roll(wide, HD // 2, 1) * sine).astype(jnp.bfloat16)


def column_of(row, width):
    pieces = []
    for at in range(0, width, LANES):
        size = min(LANES, width - at)
        eye = lax.broadcasted_iota(jnp.int32, (size, size), 0) == lax.broadcasted_iota(
            jnp.int32, (size, size), 1
        )
        pieces.append(
            jnp.sum(jnp.where(eye, row[:, at : at + size], 0.0), axis=1, keepdims=True)
        )
    return jnp.concatenate(pieces, axis=0)


def carried_tokens(mine, own, earlier):
    count = jnp.zeros((1, 1), jnp.float32)
    for back, row in enumerate(earlier, 1):
        same = jnp.where(row == own[:, :1], 1.0, 0.0)
        here = jnp.sum(same, axis=1, keepdims=True)
        count = count + jnp.where(mine >= back, here, 0.0)
    return count


def row_places(size):
    return lax.broadcasted_iota(jnp.int32, (size, 1), 0).astype(jnp.float32)


def lane_places(size):
    return lax.broadcasted_iota(jnp.int32, (1, size), 1).astype(jnp.float32)


def scores_of(query, keys):
    return lax.dot_general(
        query, keys, (((1,), (1,)), ((), ())), preferred_element_type=jnp.float32
    )


def group_rows(head, tile, rows):
    return [
        pl.ds((head * GROUP + g) * rows + tile * TILE, TILE) for g in range(GROUP)
    ]


def own_kernel(hops, rows, *refs):
    mine_ref, freq_hbm, own_hbm = refs[:3]
    earlier_refs = refs[3 : 3 + hops]
    query_hbm, key_hbm, value_hbm = refs[3 + hops : 6 + hops]
    rot_ref, total_ref, top_ref, denom_ref, info_ref = refs[6 + hops : 11 + hops]
    freq_ref, own_ref, query_ref, key_ref, value_ref, bias_ref, sems = refs[11 + hops :]
    first_copies = [
        pltpu.make_async_copy(own_hbm, own_ref, sems.at[3]),
        pltpu.make_async_copy(freq_hbm, freq_ref, sems.at[4]),
    ]
    copies = [
        pltpu.make_async_copy(key_hbm, key_ref, sems.at[0]),
        pltpu.make_async_copy(value_hbm, value_ref, sems.at[1]),
        pltpu.make_async_copy(query_hbm, query_ref, sems.at[2]),
    ]
    for copy in first_copies + copies:
        copy.start()
    for copy in first_copies:
        copy.wait()
    own = own_ref[...].astype(jnp.float32)
    carry = carried_tokens(
        mine_ref[0], own, [ref[...].astype(jnp.float32) for ref in earlier_refs]
    )
    inside = jnp.sum(jnp.where(own == own[:, :1], 1.0, 0.0), axis=1, keepdims=True)
    inside = jnp.where(carry > 0.0, inside, 0.0)
    info_ref[0:1, :] = freq_ref[...]
    info_ref[1:2, :] = jnp.broadcast_to(carry, (1, HD))
    info_ref[2:3, :] = jnp.broadcast_to(inside, (1, HD))
    column = column_of(own, rows)
    first = jnp.sum(jnp.where(own < column, 1.0, 0.0), axis=1, keepdims=True)
    place = row_places(rows)
    positions = place - first + jnp.where(first == 0.0, carry, 0.0)
    cosine, sine = rope_factors(positions, freq_ref[...])
    key_place = lane_places(rows)
    live = (key_place >= first) & (key_place <= place)
    bias_ref[...] = jnp.where(live, 0.0, DEAD)
    for copy in copies:
        copy.wait()

    units = [(head, tile) for head in range(HK) for tile in range(rows // TILE)]
    keys_of = {}

    def start(unit):
        head, tile = unit
        span = slice(tile * TILE, (tile + 1) * TILE)
        if head not in keys_of:
            keys_of[head] = turned(key_ref[:, head * HD : (head + 1) * HD], cosine, sine)
        parts = []
        for g, at in enumerate(group_rows(head, tile, rows)):
            lanes = slice((head * GROUP + g) * HD, (head * GROUP + g + 1) * HD)
            part = turned(query_ref[span, lanes], cosine[span], sine[span])
            rot_ref[at, :] = part
            parts.append(part)
        return scores_of(jnp.concatenate(parts, axis=0), keys_of[head][: (tile + 1) * TILE])

    def finish(unit, scores):
        head, tile = unit
        seen = (tile + 1) * TILE
        bias = bias_ref[tile * TILE : (tile + 1) * TILE, :seen]
        scores = scores.reshape(GROUP, TILE, seen) + bias[None]
        scores = scores.reshape(GROUP * TILE, seen)
        top = jnp.max(scores, axis=1, keepdims=True)
        weights = jnp.exp2((scores - top) * SCALE)
        denom = jnp.sum(weights, axis=1, keepdims=True)
        total = jnp.dot(
            weights.astype(jnp.bfloat16),
            value_ref[:seen, head * HD : (head + 1) * HD],
            preferred_element_type=jnp.float32,
        )
        top = jnp.broadcast_to(top, total.shape)
        denom = jnp.broadcast_to(denom, total.shape)
        for g, at in enumerate(group_rows(head, tile, rows)):
            piece = slice(g * TILE, (g + 1) * TILE)
            total_ref[at, :] = total[piece]
            top_ref[at, :] = top[piece]
            denom_ref[at, :] = denom[piece]

    waiting = start(units[0])
    for now, later in zip(units, units[1:] + [None]):
        following = start(later) if later is not None else None
        finish(now, waiting)
        waiting = following


def earlier_kernel(hops, rows, table, *refs):
    held = len(refs) - 11
    mine_ref, rot_ref, total_ref, top_ref, denom_ref, info_ref = refs[:6]
    block_refs = refs[6 : 6 + held]
    out_hbm, out_ref, cos_ref, sin_ref, sems = refs[6 + held :]
    mine = mine_ref[0]
    window = hops * rows
    freq = info_ref[0:1, :]
    carry = info_ref[1:2, :1]
    inside = info_ref[2:3, :1]
    cosine, sine = rope_factors(carry - window + row_places(window), freq)
    cos_ref[...] = cosine
    sin_ref[...] = sine
    key_bias = jnp.where(carry - window + lane_places(window) >= 0.0, 0.0, DEAD)

    def block(distance, lanes):
        picked = None
        for at, ref in enumerate(block_refs):
            users = [i for i in range(len(table)) if table[i].get(distance) == at]
            if not users:
                continue
            part = ref[:, lanes]
            if picked is None:
                picked = part
            else:
                wanted = functools.reduce(jnp.logical_or, [mine == i for i in users])
                picked = jnp.where(wanted, part, picked)
        return picked

    blocks_of = {}

    def start(unit):
        head, tile = unit
        if head not in blocks_of:
            keys, values = [], []
            for distance in range(hops, 0, -1):
                at = (hops - distance) * rows
                lanes = slice(head * HD, (head + 1) * HD)
                keys.append(
                    turned(
                        block(distance, lanes),
                        cos_ref[at : at + rows, :],
                        sin_ref[at : at + rows, :],
                    )
                )
                lanes = slice((HK + head) * HD, (HK + head + 1) * HD)
                values.append(block(distance, lanes))
            blocks_of[head] = (jnp.concatenate(keys, axis=0), jnp.concatenate(values, axis=0))
        query = jnp.concatenate([rot_ref[at, :] for at in group_rows(head, tile, rows)], axis=0)
        return scores_of(query, blocks_of[head][0][tile * TILE :])

    def finish(unit, scores):
        head, tile = unit
        spans = group_rows(head, tile, rows)
        live = row_places(TILE) + tile * TILE < inside
        live = jnp.concatenate([live] * GROUP, axis=0)
        scores = scores + key_bias[:, tile * TILE :]
        top = jnp.max(scores, axis=1, keepdims=True)
        old = jnp.concatenate([top_ref[at, :] for at in spans], axis=0)
        new = jnp.maximum(old, jnp.where(live, top, DEAD))
        shift = jnp.where(live, new, -DEAD)[:, :1]
        weights = jnp.exp2((scores - shift) * SCALE)
        denom = jnp.sum(weights, axis=1, keepdims=True)
        part = jnp.dot(
            weights.astype(jnp.bfloat16),
            blocks_of[head][1][tile * TILE :],
            preferred_element_type=jnp.float32,
        )
        rescale = jnp.exp2((old - new) * SCALE)
        old_denom = jnp.concatenate([denom_ref[at, :] for at in spans], axis=0)
        old_total = jnp.concatenate([total_ref[at, :] for at in spans], axis=0)
        result = (old_total * rescale + part) / (old_denom * rescale + denom)
        result = result.astype(jnp.bfloat16)
        for g in range(GROUP):
            lanes = slice((head * GROUP + g) * HD, (head * GROUP + g + 1) * HD)
            out_ref[tile * TILE : (tile + 1) * TILE, lanes] = result[
                g * TILE : (g + 1) * TILE
            ]

    units = [(head, tile) for head in range(HK) for tile in range(rows // TILE)]
    copies = []
    waiting = start(units[0])
    for now, later in zip(units, units[1:] + [None]):
        following = start(later) if later is not None else None
        finish(now, waiting)
        waiting = following
        if later is None or later[0] != now[0]:
            lanes = pl.ds(now[0] * GROUP * HD, GROUP * HD)
            copy = pltpu.make_async_copy(
                out_ref.at[:, lanes], out_hbm.at[:, lanes], sems.at[now[0]]
            )
            copy.start()
            copies.append(copy)
    for copy in copies:
        copy.wait()


def plan_rounds(size, hops):
    wanted = [(i, i + 2) for i in range(1, size - 2, 2)]
    wanted += [(i, i + 1) for i in range(0, size - 1, 2)]
    wanted += [(i, i + 2) for i in range(0, size - 2, 2)]
    for distance in range(3, hops + 1):
        wanted += [(i, i + distance) for i in range(size - distance)]
    if hops == 1:
        wanted = [(i, i + 1) for i in range(size - 1)]
    rounds, table = [], [{} for _ in range(size)]
    for source, target in wanted:
        at = 0
        while at < len(rounds) and any(s == source or t == target for s, t in rounds[at]):
            at += 1
        if at == len(rounds):
            rounds.append([])
        rounds[at].append((source, target))
        table[target][target - source] = at
    forward = []
    if hops > 1:
        for i in range(2, size, 2):
            forward.append((i + 1, i))
            table[i][1] = len(rounds)
    return rounds, forward, table


def body(queries, keys, values, segments):
    rows = segments.shape[1]
    size = lax.axis_size("ctx")
    hops = size // 2
    mine = lax.axis_index("ctx").astype(jnp.int32).reshape(1)
    rounds, forward, table = plan_rounds(size, hops)

    packed = jnp.concatenate([keys[0], values[0]], axis=1)
    with jax.named_scope("cross"):
        blocks = [lax.ppermute(packed, "ctx", pairs) for pairs in rounds]
    with jax.named_scope("numbers"):
        earlier = [
            lax.ppermute(segments, "ctx", [(i, i + d) for i in range(size - d)])
            for d in range(1, hops + 1)
        ]
    freq = jnp.asarray(frequencies())
    vmem = pl.BlockSpec(memory_space=pltpu.VMEM)
    smem = pl.BlockSpec(memory_space=pltpu.SMEM)
    hbm = pl.BlockSpec(memory_space=pltpu.HBM)
    state = jax.ShapeDtypeStruct((HQ * rows, HD), jnp.float32)
    pairs = HQ * rows * rows
    info = jax.ShapeDtypeStruct((8, HD), jnp.float32)
    rot, total, top, denom, info = pl.pallas_call(
        functools.partial(own_kernel, hops, rows),
        out_shape=[jax.ShapeDtypeStruct((HQ * rows, HD), jnp.bfloat16), state, state, state, info],
        in_specs=[smem, hbm, hbm] + [vmem] * hops + [hbm] * 3,
        out_specs=[vmem] * 5,
        scratch_shapes=[
            pltpu.VMEM((1, HD), jnp.float32),
            pltpu.VMEM((1, rows), jnp.int32),
            pltpu.VMEM((rows, HQ * HD), jnp.bfloat16),
            pltpu.VMEM((rows, HK * HD), jnp.bfloat16),
            pltpu.VMEM((rows, HK * HD), jnp.bfloat16),
            pltpu.VMEM((rows, rows), jnp.float32),
            pltpu.SemaphoreType.DMA((5,)),
        ],
        compiler_params=pltpu.CompilerParams(vmem_limit_bytes=(12 + 4 * hops) << 20),
        cost_estimate=pl.CostEstimate(
            flops=4 * HD * pairs, bytes_accessed=4 << 20, transcendentals=pairs
        ),
        name="own",
    )(mine, freq, segments, *earlier, queries[0], keys[0], values[0])
    if forward:
        ready, rot = lax.optimization_barrier((blocks[0], rot))
        with jax.named_scope("forward"):
            blocks.append(lax.ppermute(ready, "ctx", forward))
    out = pl.pallas_call(
        functools.partial(earlier_kernel, hops, rows, table),
        out_shape=jax.ShapeDtypeStruct((rows, HQ * HD), jnp.bfloat16),
        in_specs=[smem] + [vmem] * (5 + len(blocks)),
        out_specs=hbm,
        scratch_shapes=[
            pltpu.VMEM((rows, HQ * HD), jnp.bfloat16),
            pltpu.VMEM((hops * rows, HD), jnp.float32),
            pltpu.VMEM((hops * rows, HD), jnp.float32),
            pltpu.SemaphoreType.DMA((HK,)),
        ],
        compiler_params=pltpu.CompilerParams(vmem_limit_bytes=(12 + 4 * hops) << 20),
        cost_estimate=pl.CostEstimate(
            flops=4 * HD * pairs * hops,
            bytes_accessed=4 << 20,
            transcendentals=pairs * hops,
        ),
        name="earlier",
    )(mine, rot, total, top, denom, info, *blocks)
    return out[None]


def solution(mesh):
    placed = (P("dp", "ctx", None), P("dp", "ctx", None), P("dp", "ctx", None), P("dp", "ctx"))
    return jax.shard_map(
        body, mesh=mesh, in_specs=placed, out_specs=P("dp", "ctx", None), check_vma=False
    )
```

time: 40.5 us -> 34 us (0.84)
  waiting for transfers between devices: 17.2 us -> 6.68 us
  Pallas kernels: 10.8 us -> 13.9 us
  other arithmetic: 0 us -> 1.08 us
  local copies, waits for them, and re-layouts: 3.78 us -> 4.46 us
    ppermute x6 -> x5, waiting for transfers between devices: 17.2 us -> 6.68 us  [the longest x2 5.2 us: body(): lax.ppermute(segments, 'ctx', [(i, i + d) for i in range(size - d)])]
    pallas_call x1 -> x2, Pallas kernels: 10.8 us -> 13.9 us  [the longest x1 10.9 us: body(): pl.pallas_call(functools.partial(earlier_kernel, hops, rows, table), out_...]
    concatenate x0 -> x1, other arithmetic: none -> 1.08 us  [body(): packed = jnp.concatenate([keys[0], values[0]], axis=1)]
    unnamed x10, local copies, waits for them, and re-layouts: 3.78 us -> 4.46 us
    ppermute x6 -> x5, starting transfers between devices: 7.86 us -> 7.48 us  [the longest x2 2.58 us: body(): blocks = [lax.ppermute(packed, 'ctx', pairs) for pairs in rounds]]
  transfers between devices with their start and end apart: 6 -> 5, of which waited for: 2 -> 2; matrix products, arithmetic and copies ran while one was open for 0% -> 0% of each run, Pallas kernels for 0% -> 9%
where the time goes in v2:
time: 34 us; the launch traced here: 33.6 us
  Pallas kernels  13.9 us (41%)
  starting transfers between devices  7.48 us (22%)
  waiting for transfers between devices  6.68 us (20%)
  local copies, waits for them, and re-layouts  4.46 us (13%)
  other arithmetic  1.08 us (3%)
    pallas_call x1, Pallas kernels, body(): pl.pallas_call(functools.partial(earlier_kernel, hops, rows, table), out_...  10.9 us
    ppermute x2, waiting for transfers between devices, body(): lax.ppermute(segments, 'ctx', [(i, i + d) for i in range(size - d)])  5.2 us
    unnamed x10, local copies, waits for them, and re-layouts  4.46 us
    pallas_call x1, Pallas kernels, body(): pl.pallas_call(functools.partial(own_kernel, hops, rows), out_shape=[jax....  2.92 us
    ppermute x2, starting transfers between devices, body(): blocks = [lax.ppermute(packed, 'ctx', pairs) for pairs in rounds]  2.58 us
    ppermute x2, starting transfers between devices, body(): lax.ppermute(segments, 'ctx', [(i, i + d) for i in range(size - d)])  2.58 us
    ppermute x1, starting transfers between devices, body(): blocks.append(lax.ppermute(ready, 'ctx', forward))  2.31 us
    ppermute x1, waiting for transfers between devices, body(): blocks.append(lax.ppermute(ready, 'ctx', forward))  1.48 us
  transfers between devices with their start and end apart: 5, of which 2 were waited for; matrix products, arithmetic and copies ran while one was open for 0% of the time, Pallas kernels for 9%

profile of v2, /device:TPU:21, one launch (start us, length us, event | category | flops | bytes accessed | tf_op | source)
XLA Modules:
  0.0 33.6 jit_solution(1177320650307570583)
XLA Ops:
  0.0 1.1 %pad_maximum_fusion = bf16[256,1024]{1,0:T(8,128)(2,1)S(1)} fusion(bf16[256,512]{1,0:T(8,128)(2,1)} %bitcast.7, bf16[256,512]{1,0:T(8,128)(2,1)} %bitcast.5), kind=kLoop, calls=%fused_computation | loop fusion | flops 1048576 | bytes 1048576 | tf_op jit(solution)/shard_map/concatenate | solution.py:317
  1.1 1.3 %collective-permute-start = (bf16[256,1024]{1,0:T(8,128)(2,1)S(1)}, bf16[256,1024]{1,0:T(8,128)(2,1)S(1)}, u32[]{:S(2)}, u32[]{:S(2)}) collective-permute-start(bf16[256,1024]{1,0:T(8,128)(2,1)S(1)} %pad_maximum_fusion), channel_id=1, source_target_pairs={{1,3},{0,1},{5,7},{4,5},{9,11},{8,9},{13,15},{12,13},{17,19},{16,1... | collective-permute-start | bytes 1572872 | tf_op jit(solution)/shard_map/cross/ppermute | solution.py:319
  2.4 1.3 %collective-permute-start.1 = (s32[1,256]{1,0:T(1,128)}, s32[1,256]{1,0:T(1,128)S(1)}, u32[]{:S(2)}, u32[]{:S(2)}) collective-permute-start(s32[1,256]{1,0:T(1,128)} %refs_2_.1), channel_id=1, source_target_pairs={{0,1},{1,2},{2,3},{4,5},{5,6},{6,7},{8,9},{9,10},{10,11},{12,13},{... | collective-permute-start | bytes 3080 | tf_op jit(solution)/shard_map/numbers/ppermute | solution.py:322
  3.7 1.3 %collective-permute-start.2 = (s32[1,256]{1,0:T(1,128)}, s32[1,256]{1,0:T(1,128)S(1)}, u32[]{:S(2)}, u32[]{:S(2)}) collective-permute-start(s32[1,256]{1,0:T(1,128)} %refs_2_.1), channel_id=1, source_target_pairs={{0,2},{1,3},{4,6},{5,7},{8,10},{9,11},{12,14},{13,15},{16,18},{17,... | collective-permute-start | bytes 3080 | tf_op jit(solution)/shard_map/numbers/ppermute | solution.py:322
  5.0 1.3 %collective-permute-start.3 = (bf16[256,1024]{1,0:T(8,128)(2,1)S(1)}, bf16[256,1024]{1,0:T(8,128)(2,1)S(1)}, u32[]{:S(2)}, u32[]{:S(2)}) collective-permute-start(bf16[256,1024]{1,0:T(8,128)(2,1)S(1)} %pad_maximum_fusion), channel_id=1, source_target_pairs={{2,3},{0,2},{6,7},{4,6},{10,11},{8,10},{14,15},{12,14},{18,19},{16... | collective-permute-start | bytes 1572872 | tf_op jit(solution)/shard_map/cross/ppermute | solution.py:319
  6.3 0.0 collective-permute-done.1.refs_3_
  6.3 5.2 %collective-permute-done.2.refs_4_ = s32[1,256]{1,0:T(1,128)S(1)} collective-permute-done((s32[1,256]{1,0:T(1,128)}, s32[1,256]{1,0:T(1,128)S(1)}, u32[]{:S(2)}, u32[]{:S(2)}) %collective-permute-start.2) | collective-permute-done | bytes 1056 | tf_op jit(solution)/shard_map/numbers/ppermute | solution.py:322
  11.5 0.0 copy-start
  11.5 0.9 %copy-done = bf16[1,256,512]{2,1,0:T(8,128)(2,1)S(1)} copy-done((bf16[1,256,512]{2,1,0:T(8,128)(2,1)S(1)}, bf16[1,256,512]{2,1,0:T(8,128)(2,1)}, u32[]{:S(2)}) %copy-start) | copy-done | bytes 262168
  12.4 0.0 copy-start.1
  12.5 0.9 %copy-done.1 = bf16[1,256,512]{2,1,0:T(8,128)(2,1)S(1)} copy-done((bf16[1,256,512]{2,1,0:T(8,128)(2,1)S(1)}, bf16[1,256,512]{2,1,0:T(8,128)(2,1)}, u32[]{:S(2)}) %copy-start.1) | copy-done | bytes 262168
  13.4 0.0 copy-start.2
  13.4 1.2 %copy-done.2 = bf16[1,256,2048]{2,1,0:T(8,128)(2,1)S(1)} copy-done((bf16[1,256,2048]{2,1,0:T(8,128)(2,1)S(1)}, bf16[1,256,2048]{2,1,0:T(8,128)(2,1)}, u32[]{:S(2)}) %copy-start.2) | copy-done | bytes 1048600
  14.6 0.0 copy-start.3
  14.6 0.7 %copy-done.3 = s32[1,256]{1,0:T(1,128)S(1)} copy-done((s32[1,256]{1,0:T(1,128)S(1)}, s32[1,256]{1,0:T(1,128)}, u32[]{:S(2)}) %copy-start.3) | copy-done | bytes 1048
  15.3 0.0 copy-start.4
  15.3 0.7 %copy-done.4 = f32[1,128]{1,0:T(1,128)S(1)} copy-done((f32[1,128]{1,0:T(1,128)S(1)}, f32[1,128]{1,0:T(1,128)}, u32[]{:S(2)}) %copy-start.4) | copy-done | bytes 536
  16.0 2.9 %own.1 = (bf16[4096,128]{1,0:T(8,128)(2,1)S(1)}, f32[4096,128]{1,0:T(8,128)S(1)}, f32[4096,128]{1,0:T(8,128)S(1)}, f32[4096,128]{1,0:T(8,128)S(1)}, f32[8,128]{1,0:T(8,128)S(1)}) custom-call(s32[1]{0:T(128)} %bitcast.refs_0_, f32[1,128]{1,0:T(1,128)S(1)} %copy-done.4, s32[1,256]{1,0:T(1,128)S(1)} %copy-done.3, s32[1,256]{1,0:T(1,128)S(1)} %collective-permute-done.1.refs_3_, ...), custom_call_target="tpu_custom_call" | custom-call | flops 536870912 | bytes 4194304 | tf_op jit(solution)/shard_map/own/pallas_call | solution.py:332
  18.9 0.0 collective-permute-done.refs_6_
  18.9 2.3 %collective-permute-start.4 = (bf16[256,1024]{1,0:T(8,128)(2,1)S(1)}, bf16[256,1024]{1,0:T(8,128)(2,1)S(1)}, u32[]{:S(2)}, u32[]{:S(2)}) collective-permute-start(bf16[256,1024]{1,0:T(8,128)(2,1)S(1)} %collective-permute-done.refs_6_), channel_id=1, source_target_pairs={{3,2},{7,6},{11,10},{15,14},{19,18},{23,22},{27,26},{31,30}} | collective-permute-start | bytes 1572872 | tf_op jit(solution)/shard_map/forward/ppermute | solution.py:355
  21.2 0.0 collective-permute-done.3.refs_7_
  21.2 1.5 %collective-permute-done.4.refs_8_ = bf16[256,1024]{1,0:T(8,128)(2,1)S(1)} collective-permute-done((bf16[256,1024]{1,0:T(8,128)(2,1)S(1)}, bf16[256,1024]{1,0:T(8,128)(2,1)S(1)}, u32[]{:S(2)}, u32[]{:S(2)}) %collective-permute-start.4) | collective-permute-done | bytes 524320 | tf_op jit(solution)/shard_map/forward/ppermute | solution.py:355
  22.7 10.9 %earlier.1 = bf16[256,2048]{1,0:T(8,128)(2,1)} custom-call(s32[1]{0:T(128)} %bitcast.refs_0_, bf16[4096,128]{1,0:T(8,128)(2,1)S(1)} %get-tuple-element.13.refs_1_, f32[4096,128]{1,0:T(8,128)S(1)} %get-tuple-element.14.refs_2_, f32[4096,128]{1,0:T(8,128)S(1)} %get-tuple-element.15.refs_3_, f32[4096,128]{1,0:T(8,128)S(1)} %get-tuple-element.16.refs_4_, ...), custom_call_target="tpu_custom_call" | custom-call | flops 1073741824 | bytes 4194304 | tf_op jit(solution)/shard_map/earlier/pallas_call | solution.py:356
Async XLA Ops:
  1.1 17.8 %collective-permute-start = (bf16[256,1024]{1,0:T(8,128)(2,1)S(1)}, bf16[256,1024]{1,0:T(8,128)(2,1)S(1)}, u32[]{:S(2)}, u32[]{:S(2)}) collective-permute-start(bf16[256,1024]{1,0:T(8,128)(2,1)S(1)} %pad_maximum_fusion), channel_id=1, source_target_pairs={{1,3},{0,1},{5,7},{4,5},{9,11},{8,9},{13,15},{12,13},{17,19},{16,1... | collective-permute-start | bytes 1572872 | tf_op jit(solution)/shard_map/cross/ppermute | solution.py:319
  2.4 3.9 %collective-permute-start.1 = (s32[1,256]{1,0:T(1,128)}, s32[1,256]{1,0:T(1,128)S(1)}, u32[]{:S(2)}, u32[]{:S(2)}) collective-permute-start(s32[1,256]{1,0:T(1,128)} %refs_2_.1), channel_id=1, source_target_pairs={{0,1},{1,2},{2,3},{4,5},{5,6},{6,7},{8,9},{9,10},{10,11},{12,13},{... | collective-permute-start | bytes 3080 | tf_op jit(solution)/shard_map/numbers/ppermute | solution.py:322
  3.7 7.8 %collective-permute-start.2 = (s32[1,256]{1,0:T(1,128)}, s32[1,256]{1,0:T(1,128)S(1)}, u32[]{:S(2)}, u32[]{:S(2)}) collective-permute-start(s32[1,256]{1,0:T(1,128)} %refs_2_.1), channel_id=1, source_target_pairs={{0,2},{1,3},{4,6},{5,7},{8,10},{9,11},{12,14},{13,15},{16,18},{17,... | collective-permute-start | bytes 3080 | tf_op jit(solution)/shard_map/numbers/ppermute | solution.py:322
  5.0 16.2 %collective-permute-start.3 = (bf16[256,1024]{1,0:T(8,128)(2,1)S(1)}, bf16[256,1024]{1,0:T(8,128)(2,1)S(1)}, u32[]{:S(2)}, u32[]{:S(2)}) collective-permute-start(bf16[256,1024]{1,0:T(8,128)(2,1)S(1)} %pad_maximum_fusion), channel_id=1, source_target_pairs={{2,3},{0,2},{6,7},{4,6},{10,11},{8,10},{14,15},{12,14},{18,19},{16... | collective-permute-start | bytes 1572872 | tf_op jit(solution)/shard_map/cross/ppermute | solution.py:319
  11.5 1.0 %copy-start = (bf16[1,256,512]{2,1,0:T(8,128)(2,1)S(1)}, bf16[1,256,512]{2,1,0:T(8,128)(2,1)}, u32[]{:S(2)}) copy-start(bf16[1,256,512]{2,1,0:T(8,128)(2,1)} %param.6) | copy-start | bytes 786436
  12.4 0.9 %copy-start.1 = (bf16[1,256,512]{2,1,0:T(8,128)(2,1)S(1)}, bf16[1,256,512]{2,1,0:T(8,128)(2,1)}, u32[]{:S(2)}) copy-start(bf16[1,256,512]{2,1,0:T(8,128)(2,1)} %param.7) | copy-start | bytes 786436
  13.4 1.2 %copy-start.2 = (bf16[1,256,2048]{2,1,0:T(8,128)(2,1)S(1)}, bf16[1,256,2048]{2,1,0:T(8,128)(2,1)}, u32[]{:S(2)}) copy-start(bf16[1,256,2048]{2,1,0:T(8,128)(2,1)} %param.5) | copy-start | bytes 3145732
  14.6 0.7 %copy-start.3 = (s32[1,256]{1,0:T(1,128)S(1)}, s32[1,256]{1,0:T(1,128)}, u32[]{:S(2)}) copy-start(s32[1,256]{1,0:T(1,128)} %refs_2_.1) | copy-start | bytes 3076
  15.3 0.7 %copy-start.4 = (f32[1,128]{1,0:T(1,128)S(1)}, f32[1,128]{1,0:T(1,128)}, u32[]{:S(2)}) copy-start(f32[1,128]{1,0:T(1,128)} %constant.6.clone.refs_1_) | copy-start | bytes 1540
  18.9 3.8 %collective-permute-start.4 = (bf16[256,1024]{1,0:T(8,128)(2,1)S(1)}, bf16[256,1024]{1,0:T(8,128)(2,1)S(1)}, u32[]{:S(2)}, u32[]{:S(2)}) collective-permute-start(bf16[256,1024]{1,0:T(8,128)(2,1)S(1)} %collective-permute-done.refs_6_), channel_id=1, source_target_pairs={{3,2},{7,6},{11,10},{15,14},{19,18},{23,22},{27,26},{31,30}} | collective-permute-start | bytes 1572872 | tf_op jit(solution)/shard_map/forward/ppermute | solution.py:355

commit v3 on v2

v3 whole, which is shorter than its diff:
```python
import functools
import math

import jax
import jax.numpy as jnp
import numpy as np
from jax import lax
from jax.experimental import pallas as pl
from jax.experimental.pallas import tpu as pltpu
from jax.sharding import PartitionSpec as P

HQ = 16
HK = 4
HD = 128
GROUP = HQ // HK
ROPE_THETA = 500000.0
LANES = 128
DEAD = -1e30


def frequencies():
    half = HD // 2
    steps = np.arange(half, dtype=np.float32)
    log_theta = np.log(np.float32(ROPE_THETA))
    return np.exp(-log_theta * np.float32(2.0) * steps / np.float32(HD)).astype(np.float32)


def frequency_row():
    lane = lax.broadcasted_iota(jnp.int32, (1, HD), 1)
    lane = jnp.where(lane < HD // 2, lane, lane - HD // 2)
    row = jnp.zeros((1, HD), jnp.float32)
    for at, freq in enumerate(frequencies()):
        row = jnp.where(lane == at, float(freq), row)
    return row


TURN = 2.0 * math.pi
TURN_HIGH = 6.28125
TURN_MID = float(np.float32(np.round((TURN - TURN_HIGH) * 2**22) / 2**22))
TURN_LOW = TURN - TURN_HIGH - TURN_MID
SIN_TERMS = [(-1.0) ** n * TURN ** (2 * n + 1) / math.factorial(2 * n + 1) for n in range(7)]
SCALE = math.log2(math.e) / math.sqrt(HD)
TILE = 128


def rope_factors(positions, freq):
    angle = positions * freq
    whole = jnp.round(angle * (1.0 / TURN))
    rest = ((angle - whole * TURN_HIGH) - whole * TURN_MID) - whole * TURN_LOW
    turns = rest * (1.0 / TURN)
    lane = lax.broadcasted_iota(jnp.int32, freq.shape, 1)
    low = lane < HD // 2
    turns = turns - jnp.where(low, 0.0, 0.25)
    turns = turns - jnp.round(turns)
    part = 0.25 - jnp.abs(turns)
    square = part * part
    total = jnp.full_like(square, SIN_TERMS[-1])
    for term in SIN_TERMS[-2::-1]:
        total = total * square + term
    both = total * part
    swapped = pltpu.roll(both, HD // 2, 1)
    return jnp.where(low, both, swapped), jnp.where(low, -swapped, both)


def turned(rows, cosine, sine):
    wide = rows.astype(jnp.float32)
    return (wide * cosine + pltpu.roll(wide, HD // 2, 1) * sine).astype(jnp.bfloat16)


def column_of(row, width):
    pieces = []
    for at in range(0, width, LANES):
        size = min(LANES, width - at)
        eye = lax.broadcasted_iota(jnp.int32, (size, size), 0) == lax.broadcasted_iota(
            jnp.int32, (size, size), 1
        )
        pieces.append(
            jnp.sum(jnp.where(eye, row[:, at : at + size], 0.0), axis=1, keepdims=True)
        )
    return jnp.concatenate(pieces, axis=0)


def carried_tokens(mine, own, earlier):
    count = jnp.zeros((1, 1), jnp.float32)
    for back, row in enumerate(earlier, 1):
        same = jnp.where(row == own[:, :1], 1.0, 0.0)
        here = jnp.sum(same, axis=1, keepdims=True)
        count = count + jnp.where(mine >= back, here, 0.0)
    return count


def row_places(size):
    return lax.broadcasted_iota(jnp.int32, (size, 1), 0).astype(jnp.float32)


def lane_places(size):
    return lax.broadcasted_iota(jnp.int32, (1, size), 1).astype(jnp.float32)


def scores_of(keys, query):
    return lax.dot_general(
        keys, query, (((1,), (1,)), ((), ())), preferred_element_type=jnp.float32
    )


def flipped(block):
    return jnp.transpose(block)


def pipelined(units, start, finish):
    waiting = start(units[0])
    for now, later in zip(units, units[1:] + [None]):
        following = start(later) if later is not None else None
        finish(now, waiting)
        waiting = following


def own_kernel(hops, rows, *refs):
    mine_ref, own_ref = refs[:2]
    earlier_refs = refs[2 : 2 + hops]
    query_ref, block_ref = refs[2 + hops : 4 + hops]
    rot_ref, total_ref, top_ref, denom_ref, info_ref, bias_ref = refs[4 + hops :]
    own = own_ref[...].astype(jnp.float32)
    carry = carried_tokens(
        mine_ref[0], own, [ref[...].astype(jnp.float32) for ref in earlier_refs]
    )
    inside = jnp.sum(jnp.where(own == own[:, :1], 1.0, 0.0), axis=1, keepdims=True)
    inside = jnp.where(carry > 0.0, inside, 0.0)
    info_ref[0:1, :] = jnp.broadcast_to(carry, (1, HD))
    info_ref[1:2, :] = jnp.broadcast_to(inside, (1, HD))
    column = column_of(own, rows)
    first = jnp.sum(jnp.where(own < column, 1.0, 0.0), axis=1, keepdims=True)
    place = row_places(rows)
    positions = place - first + jnp.where(first == 0.0, carry, 0.0)
    cosine, sine = rope_factors(positions, frequency_row())
    first_row = jnp.sum(jnp.where(column < own, 1.0, 0.0), axis=0, keepdims=True)
    live = (place >= first_row) & (place <= lane_places(rows))
    bias_ref[...] = jnp.where(live, 0.0, DEAD)
    held = {}

    def start(unit):
        head = unit // GROUP
        if head not in held:
            lanes = slice(head * HD, (head + 1) * HD)
            keys = turned(block_ref[:, lanes], cosine, sine)
            lanes = slice((HK + head) * HD, (HK + head + 1) * HD)
            held[head] = (keys, flipped(block_ref[:, lanes]))
        at = slice(unit * rows, (unit + 1) * rows)
        query = turned(query_ref[:, unit * HD : (unit + 1) * HD], cosine, sine)
        rot_ref[at, :] = query
        return scores_of(held[head][0], query)

    def finish(unit, scores):
        pieces, tops, denoms = [], [], []
        for tile in range(rows // TILE):
            seen = (tile + 1) * TILE
            lanes = slice(tile * TILE, seen)
            part = scores[:seen, lanes] + bias_ref[:seen, lanes]
            top = jnp.max(part, axis=0, keepdims=True)
            weights = jnp.exp2((part - top) * SCALE)
            denoms.append(jnp.sum(weights, axis=0, keepdims=True))
            tops.append(top)
            weights = weights.astype(jnp.bfloat16)
            if seen < rows:
                rest = jnp.zeros((rows - seen, TILE), jnp.bfloat16)
                weights = jnp.concatenate([weights, rest], axis=0)
            pieces.append(weights)
        weights = jnp.concatenate(pieces, axis=1)
        total = jnp.dot(held[unit // GROUP][1], weights, preferred_element_type=jnp.float32)
        total_ref[unit * HD : (unit + 1) * HD, :] = total
        top_ref[unit : unit + 1, :] = jnp.concatenate(tops, axis=1)
        denom_ref[unit : unit + 1, :] = jnp.concatenate(denoms, axis=1)

    pipelined(list(range(HQ)), start, finish)


def earlier_kernel(hops, rows, table, *refs):
    held = len(refs) - 13
    mine_ref, rot_ref, total_ref, top_ref, denom_ref, info_ref = refs[:6]
    block_refs = refs[6 : 6 + held]
    out_hbm, out_ref, cos_ref, sin_ref, key_side_ref, query_side_ref, sems = refs[6 + held :]
    mine = mine_ref[0]
    window = hops * rows
    carry = info_ref[0:1, :1]
    inside = info_ref[1:2, :1]
    key_positions = carry - window + row_places(window)
    cosine, sine = rope_factors(key_positions, frequency_row())
    cos_ref[...] = cosine
    sin_ref[...] = sine
    lane = lane_places(HD)
    key_bias = jnp.where(key_positions >= 0.0, 0.0, DEAD)
    key_side = jnp.where(lane == 0.0, key_bias, jnp.where(lane == 1.0, 1.0, 0.0))
    key_side_ref[...] = key_side.astype(jnp.bfloat16)
    query_bias = jnp.where(row_places(rows) < inside, 0.0, DEAD)
    query_side = jnp.where(lane == 0.0, 1.0, jnp.where(lane == 1.0, query_bias, 0.0))
    query_side_ref[...] = query_side.astype(jnp.bfloat16)

    def block(distance, lanes):
        picked = None
        for at, ref in enumerate(block_refs):
            users = [i for i in range(len(table)) if table[i].get(distance) == at]
            if not users:
                continue
            part = ref[:, lanes]
            if picked is None:
                picked = part
            else:
                wanted = functools.reduce(jnp.logical_or, [mine == i for i in users])
                picked = jnp.where(wanted, part, picked)
        return picked

    blocks_of = {}
    copies = []

    def start(unit):
        head = unit // GROUP
        if head not in blocks_of:
            keys, values = [], []
            for distance in range(hops, 0, -1):
                at = (hops - distance) * rows
                lanes = slice(head * HD, (head + 1) * HD)
                keys.append(
                    turned(
                        block(distance, lanes),
                        cos_ref[at : at + rows, :],
                        sin_ref[at : at + rows, :],
                    )
                )
                lanes = slice((HK + head) * HD, (HK + head + 1) * HD)
                values.append(flipped(block(distance, lanes)))
            keys = jnp.concatenate([jnp.concatenate(keys, axis=0), key_side_ref[...]], axis=1)
            blocks_of[head] = (keys, jnp.concatenate(values, axis=1))
        query = rot_ref[unit * rows : (unit + 1) * rows, :]
        query = jnp.concatenate([query, query_side_ref[...]], axis=1)
        return scores_of(blocks_of[head][0], query)

    def finish(unit, scores):
        head = unit // GROUP
        pieces, rescales, denoms = [], [], []
        for tile in range(rows // TILE):
            skip = tile * TILE
            lanes = slice(skip, skip + TILE)
            part = scores[skip:, lanes]
            top = jnp.max(part, axis=0, keepdims=True)
            old = top_ref[unit : unit + 1, lanes]
            new = jnp.maximum(old, top)
            weights = jnp.exp2((part - new) * SCALE)
            rescale = jnp.exp2((old - new) * SCALE)
            denoms.append(
                denom_ref[unit : unit + 1, lanes] * rescale
                + jnp.sum(weights, axis=0, keepdims=True)
            )
            rescales.append(rescale)
            weights = weights.astype(jnp.bfloat16)
            if skip > 0:
                rest = jnp.zeros((skip, TILE), jnp.bfloat16)
                weights = jnp.concatenate([rest, weights], axis=0)
            pieces.append(weights)
        weights = jnp.concatenate(pieces, axis=1)
        part = jnp.dot(blocks_of[head][1], weights, preferred_element_type=jnp.float32)
        rescale = jnp.concatenate(rescales, axis=1)
        inverse = 1.0 / jnp.concatenate(denoms, axis=1)
        result = (total_ref[unit * HD : (unit + 1) * HD, :] * rescale + part) * inverse
        out_ref[:, unit * HD : (unit + 1) * HD] = jnp.transpose(result).astype(jnp.bfloat16)
        if unit % GROUP == GROUP - 1:
            lanes = pl.ds(head * GROUP * HD, GROUP * HD)
            copy = pltpu.make_async_copy(
                out_ref.at[:, lanes], out_hbm.at[:, lanes], sems.at[head]
            )
            copy.start()
            copies.append(copy)

    pipelined(list(range(HQ)), start, finish)
    for copy in copies:
        copy.wait()


def plan_rounds(size, hops):
    wanted = [(i, i + 2) for i in range(1, size - 2, 2)]
    wanted += [(i, i + 1) for i in range(0, size - 1, 2)]
    wanted += [(i, i + 2) for i in range(0, size - 2, 2)]
    for distance in range(3, hops + 1):
        wanted += [(i, i + distance) for i in range(size - distance)]
    if hops == 1:
        wanted = [(i, i + 1) for i in range(size - 1)]
    rounds, table = [], [{} for _ in range(size)]
    for source, target in wanted:
        at = 0
        while at < len(rounds) and any(s == source or t == target for s, t in rounds[at]):
            at += 1
        if at == len(rounds):
            rounds.append([])
        rounds[at].append((source, target))
        table[target][target - source] = at
    forward = []
    if hops > 1:
        for i in range(2, size, 2):
            forward.append((i + 1, i))
            table[i][1] = len(rounds)
    return rounds, forward, table


def body(queries, keys, values, segments):
    rows = segments.shape[1]
    size = lax.axis_size("ctx")
    hops = size // 2
    mine = lax.axis_index("ctx").astype(jnp.int32).reshape(1)
    rounds, forward, table = plan_rounds(size, hops)

    packed = jnp.concatenate([keys[0], values[0]], axis=1)
    with jax.named_scope("cross"):
        blocks = [lax.ppermute(packed, "ctx", pairs) for pairs in rounds]
    with jax.named_scope("numbers"):
        earlier = [
            lax.ppermute(segments, "ctx", [(i, i + d) for i in range(size - d)])
            for d in range(1, hops + 1)
        ]
    forwarded = blocks[0]
    if forward:
        forwarded, *earlier = lax.optimization_barrier((forwarded, *earlier))
        with jax.named_scope("forward"):
            blocks.append(lax.ppermute(forwarded, "ctx", forward))
    vmem = pl.BlockSpec(memory_space=pltpu.VMEM)
    smem = pl.BlockSpec(memory_space=pltpu.SMEM)
    hbm = pl.BlockSpec(memory_space=pltpu.HBM)
    wide_queries = queries[0].astype(jnp.float32)
    per_head = jax.ShapeDtypeStruct((HQ, rows), jnp.float32)
    pairs = HQ * rows * rows
    rot, total, top, denom, info = pl.pallas_call(
        functools.partial(own_kernel, hops, rows),
        out_shape=[
            jax.ShapeDtypeStruct((HQ * rows, HD), jnp.bfloat16),
            jax.ShapeDtypeStruct((HQ * HD, rows), jnp.float32),
            per_head,
            per_head,
            jax.ShapeDtypeStruct((8, HD), jnp.float32),
        ],
        in_specs=[smem] + [vmem] * (3 + hops),
        out_specs=[vmem] * 5,
        scratch_shapes=[pltpu.VMEM((rows, rows), jnp.float32)],
        compiler_params=pltpu.CompilerParams(vmem_limit_bytes=16 << 20),
        cost_estimate=pl.CostEstimate(
            flops=4 * HD * pairs, bytes_accessed=4 << 20, transcendentals=pairs
        ),
        name="own",
    )(mine, segments.astype(jnp.float32), *earlier, wide_queries, packed)
    out = pl.pallas_call(
        functools.partial(earlier_kernel, hops, rows, table),
        out_shape=jax.ShapeDtypeStruct((rows, HQ * HD), jnp.bfloat16),
        in_specs=[smem] + [vmem] * (5 + len(blocks)),
        out_specs=hbm,
        scratch_shapes=[
            pltpu.VMEM((rows, HQ * HD), jnp.bfloat16),
            pltpu.VMEM((hops * rows, HD), jnp.float32),
            pltpu.VMEM((hops * rows, HD), jnp.float32),
            pltpu.VMEM((hops * rows, HD), jnp.bfloat16),
            pltpu.VMEM((rows, HD), jnp.bfloat16),
            pltpu.SemaphoreType.DMA((HK,)),
        ],
        compiler_params=pltpu.CompilerParams(vmem_limit_bytes=(8 + 4 * hops) << 20),
        cost_estimate=pl.CostEstimate(
            flops=4 * HD * pairs * hops,
            bytes_accessed=4 << 20,
            transcendentals=pairs * hops,
        ),
        name="earlier",
    )(mine, rot, total, top, denom, info, *blocks)
    return out[None]


def solution(mesh):
    placed = (P("dp", "ctx", None), P("dp", "ctx", None), P("dp", "ctx", None), P("dp", "ctx"))
    return jax.shard_map(
        body, mesh=mesh, in_specs=placed, out_specs=P("dp", "ctx", None), check_vma=False
    )
```

time: 34 us -> 24 us (0.71)
  Pallas kernels: 13.9 us -> 8.41 us
  local copies, waits for them, and re-layouts: 4.46 us -> 0 us
  waiting for transfers between devices: 6.68 us -> 4.53 us
  other arithmetic: 1.08 us -> 3.22 us
    pallas_call x1, Pallas kernels: 10.9 us -> 5.46 us  [body(): pl.pallas_call(functools.partial(earlier_kernel, hops, rows, table), out_...]
    unnamed x10 -> x0, local copies, waits for them, and re-layouts: 4.46 us -> none
    convert_element_type x0 -> x2, other arithmetic: none -> 2.14 us  [the longest x1 1.46 us: body(): wide_queries = queries[0].astype(jnp.float32)]
    ppermute x1, waiting for transfers between devices: 1.48 us -> 0.01 us  [body(): blocks.append(lax.ppermute(forwarded, 'ctx', forward))]
    ppermute x2, waiting for transfers between devices: 5.2 us -> 4.52 us  [body(): lax.ppermute(segments, 'ctx', [(i, i + d) for i in range(size - d)])]
  transfers between devices with their start and end apart: 5 -> 5, of which waited for: 2 -> 1; matrix products, arithmetic and copies ran while one was open for 0% -> 9% of each run, Pallas kernels for 9% -> 12%
where the time goes in v3:
time: 24 us; the launch traced here: 23.7 us
  Pallas kernels  8.41 us (35%)
  starting transfers between devices  7.47 us (31%)
  waiting for transfers between devices  4.53 us (19%)
  other arithmetic  3.22 us (13%)
    pallas_call x1, Pallas kernels, body(): pl.pallas_call(functools.partial(earlier_kernel, hops, rows, table), out_...  5.46 us
    ppermute x2, waiting for transfers between devices, body(): lax.ppermute(segments, 'ctx', [(i, i + d) for i in range(size - d)])  4.52 us
    pallas_call x1, Pallas kernels, body(): pl.pallas_call(functools.partial(own_kernel, hops, rows), out_shape=[jax....  2.95 us
    ppermute x2, starting transfers between devices, body(): blocks = [lax.ppermute(packed, 'ctx', pairs) for pairs in rounds]  2.58 us
    ppermute x2, starting transfers between devices, body(): lax.ppermute(segments, 'ctx', [(i, i + d) for i in range(size - d)])  2.58 us
    ppermute x1, starting transfers between devices, body(): blocks.append(lax.ppermute(forwarded, 'ctx', forward))  2.3 us
    convert_element_type x1, other arithmetic, body(): wide_queries = queries[0].astype(jnp.float32)  1.46 us
    concatenate x1, other arithmetic, body(): packed = jnp.concatenate([keys[0], values[0]], axis=1)  1.08 us
  transfers between devices with their start and end apart: 5, of which 1 were waited for; matrix products, arithmetic and copies ran while one was open for 9% of the time, Pallas kernels for 12%

profile of v3, /device:TPU:21, one launch (start us, length us, event | category | flops | bytes accessed | tf_op | source)
XLA Modules:
  0.0 23.7 jit_solution(13619279141976285782)
XLA Ops:
  0.0 1.1 %pad_maximum_fusion.refs_5_ = bf16[256,1024]{1,0:T(8,128)(2,1)S(1)} fusion(bf16[256,512]{1,0:T(8,128)(2,1)} %bitcast.7, bf16[256,512]{1,0:T(8,128)(2,1)} %bitcast.8), kind=kLoop, calls=%fused_computation.1 | loop fusion | flops 1048576 | bytes 1048576 | tf_op jit(solution)/shard_map/concatenate | solution.py:310
  1.1 1.3 %collective-permute-start = (bf16[256,1024]{1,0:T(8,128)(2,1)S(1)}, bf16[256,1024]{1,0:T(8,128)(2,1)S(1)}, u32[]{:S(2)}, u32[]{:S(2)}) collective-permute-start(bf16[256,1024]{1,0:T(8,128)(2,1)S(1)} %pad_maximum_fusion.refs_5_), channel_id=1, source_target_pairs={{1,3},{0,1},{5,7},{4,5},{9,11},{8,9},{13,15},{12,13},{17,19},{16,1... | collective-permute-start | bytes 1572872 | tf_op jit(solution)/shard_map/cross/ppermute | solution.py:312
  2.4 1.3 %collective-permute-start.1 = (s32[1,256]{1,0:T(1,128)}, s32[1,256]{1,0:T(1,128)S(1)}, u32[]{:S(2)}, u32[]{:S(2)}) collective-permute-start(s32[1,256]{1,0:T(1,128)} %param.7), channel_id=1, source_target_pairs={{0,1},{1,2},{2,3},{4,5},{5,6},{6,7},{8,9},{9,10},{10,11},{12,13},{... | collective-permute-start | bytes 3080 | tf_op jit(solution)/shard_map/numbers/ppermute | solution.py:315
  3.7 1.3 %collective-permute-start.2 = (s32[1,256]{1,0:T(1,128)}, s32[1,256]{1,0:T(1,128)S(1)}, u32[]{:S(2)}, u32[]{:S(2)}) collective-permute-start(s32[1,256]{1,0:T(1,128)} %param.7), channel_id=1, source_target_pairs={{0,2},{1,3},{4,6},{5,7},{8,10},{9,11},{12,14},{13,15},{16,18},{17,... | collective-permute-start | bytes 3080 | tf_op jit(solution)/shard_map/numbers/ppermute | solution.py:315
  5.0 1.3 %collective-permute-start.3 = (bf16[256,1024]{1,0:T(8,128)(2,1)S(1)}, bf16[256,1024]{1,0:T(8,128)(2,1)S(1)}, u32[]{:S(2)}, u32[]{:S(2)}) collective-permute-start(bf16[256,1024]{1,0:T(8,128)(2,1)S(1)} %pad_maximum_fusion.refs_5_), channel_id=1, source_target_pairs={{2,3},{0,2},{6,7},{4,6},{10,11},{8,10},{14,15},{12,14},{18,19},{16... | collective-permute-start | bytes 1572872 | tf_op jit(solution)/shard_map/cross/ppermute | solution.py:312
  6.3 0.7 %convert_element_type.8.refs_1_ = f32[1,256]{1,0:T(1,128)S(1)} convert(s32[1,256]{1,0:T(1,128)} %param.7) | non-fusion elementwise | flops 256 | bytes 2048 | tf_op jit(solution)/shard_map/convert_element_type | solution.py:346
  7.0 0.0 collective-permute-done.1.refs_2_
  7.0 4.5 %collective-permute-done.2.refs_3_ = s32[1,256]{1,0:T(1,128)S(1)} collective-permute-done((s32[1,256]{1,0:T(1,128)}, s32[1,256]{1,0:T(1,128)S(1)}, u32[]{:S(2)}, u32[]{:S(2)}) %collective-permute-start.2) | collective-permute-done | bytes 1056 | tf_op jit(solution)/shard_map/numbers/ppermute | solution.py:315
  11.5 0.0 collective-permute-done.refs_6_
  11.5 2.3 %collective-permute-start.4 = (bf16[256,1024]{1,0:T(8,128)(2,1)S(1)}, bf16[256,1024]{1,0:T(8,128)(2,1)S(1)}, u32[]{:S(2)}, u32[]{:S(2)}) collective-permute-start(bf16[256,1024]{1,0:T(8,128)(2,1)S(1)} %collective-permute-done.refs_6_), channel_id=1, source_target_pairs={{3,2},{7,6},{11,10},{15,14},{19,18},{23,22},{27,26},{31,30}} | collective-permute-start | bytes 1572872 | tf_op jit(solution)/shard_map/forward/ppermute | solution.py:322
  13.8 1.5 %bitcast_convert_fusion.refs_4_ = f32[256,2048]{1,0:T(8,128)S(1)} fusion(bf16[1,256,2048]{2,1,0:T(8,128)(2,1)} %param.4), kind=kLoop, calls=%fused_computation | loop fusion | flops 524288 | bytes 3145728 | tf_op jit(solution)/shard_map/convert_element_type | solution.py:326
  15.3 3.0 %own.1 = (bf16[4096,128]{1,0:T(8,128)(2,1)S(1)}, f32[2048,256]{1,0:T(8,128)S(1)}, f32[16,256]{1,0:T(8,128)S(1)}, f32[16,256]{1,0:T(8,128)S(1)}, f32[8,128]{1,0:T(8,128)S(1)}) custom-call(s32[1]{0:T(128)} %bitcast.refs_0_, f32[1,256]{1,0:T(1,128)S(1)} %convert_element_type.8.refs_1_, s32[1,256]{1,0:T(1,128)S(1)} %collective-permute-done.1.refs_2_, ...), custom_call_target="tpu_custom_call" | custom-call | flops 536870912 | bytes 4194304 | tf_op jit(solution)/shard_map/own/pallas_call | solution.py:329
  18.2 0.0 collective-permute-done.3.refs_7_
  18.2 0.0 collective-permute-done.4.refs_8_
  18.3 5.5 %earlier.1 = bf16[256,2048]{1,0:T(8,128)(2,1)} custom-call(s32[1]{0:T(128)} %bitcast.refs_0_, bf16[4096,128]{1,0:T(8,128)(2,1)S(1)} %get-tuple-element.15.refs_1_, f32[2048,256]{1,0:T(8,128)S(1)} %get-tuple-element.16.refs_2_, f32[16,256]{1,0:T(8,128)S(1)} %get-tuple-element.17.refs_3_, f32[16,256]{1,0:T(8,128)S(1)} %get-tuple-element.18.refs_4_, ...), custom_call_target="tpu_custom_call" | custom-call | flops 1073741824 | bytes 4194304 | tf_op jit(solution)/shard_map/earlier/pallas_call | solution.py:347
Async XLA Ops:
  1.1 10.4 %collective-permute-start = (bf16[256,1024]{1,0:T(8,128)(2,1)S(1)}, bf16[256,1024]{1,0:T(8,128)(2,1)S(1)}, u32[]{:S(2)}, u32[]{:S(2)}) collective-permute-start(bf16[256,1024]{1,0:T(8,128)(2,1)S(1)} %pad_maximum_fusion.refs_5_), channel_id=1, source_target_pairs={{1,3},{0,1},{5,7},{4,5},{9,11},{8,9},{13,15},{12,13},{17,19},{16,1... | collective-permute-start | bytes 1572872 | tf_op jit(solution)/shard_map/cross/ppermute | solution.py:312
  2.4 4.6 %collective-permute-start.1 = (s32[1,256]{1,0:T(1,128)}, s32[1,256]{1,0:T(1,128)S(1)}, u32[]{:S(2)}, u32[]{:S(2)}) collective-permute-start(s32[1,256]{1,0:T(1,128)} %param.7), channel_id=1, source_target_pairs={{0,1},{1,2},{2,3},{4,5},{5,6},{6,7},{8,9},{9,10},{10,11},{12,13},{... | collective-permute-start | bytes 3080 | tf_op jit(solution)/shard_map/numbers/ppermute | solution.py:315
  3.7 7.8 %collective-permute-start.2 = (s32[1,256]{1,0:T(1,128)}, s32[1,256]{1,0:T(1,128)S(1)}, u32[]{:S(2)}, u32[]{:S(2)}) collective-permute-start(s32[1,256]{1,0:T(1,128)} %param.7), channel_id=1, source_target_pairs={{0,2},{1,3},{4,6},{5,7},{8,10},{9,11},{12,14},{13,15},{16,18},{17,... | collective-permute-start | bytes 3080 | tf_op jit(solution)/shard_map/numbers/ppermute | solution.py:315
  5.0 13.2 %collective-permute-start.3 = (bf16[256,1024]{1,0:T(8,128)(2,1)S(1)}, bf16[256,1024]{1,0:T(8,128)(2,1)S(1)}, u32[]{:S(2)}, u32[]{:S(2)}) collective-permute-start(bf16[256,1024]{1,0:T(8,128)(2,1)S(1)} %pad_maximum_fusion.refs_5_), channel_id=1, source_target_pairs={{2,3},{0,2},{6,7},{4,6},{10,11},{8,10},{14,15},{12,14},{18,19},{16... | collective-permute-start | bytes 1572872 | tf_op jit(solution)/shard_map/cross/ppermute | solution.py:312
  11.5 6.7 %collective-permute-start.4 = (bf16[256,1024]{1,0:T(8,128)(2,1)S(1)}, bf16[256,1024]{1,0:T(8,128)(2,1)S(1)}, u32[]{:S(2)}, u32[]{:S(2)}) collective-permute-start(bf16[256,1024]{1,0:T(8,128)(2,1)S(1)} %collective-permute-done.refs_6_), channel_id=1, source_target_pairs={{3,2},{7,6},{11,10},{15,14},{19,18},{23,22},{27,26},{31,30}} | collective-permute-start | bytes 1572872 | tf_op jit(solution)/shard_map/forward/ppermute | solution.py:322
